TPU v7x, 128 devices: a whole 4x4x4 slice. The times are simulated.
128 devices in a mesh: row: 8 (over x, core), col: 16 (over y, z).
Axes of the slice: x: 4, y: 4, z: 4, core: 2. Of those that a mesh axis runs over, the one named last changes fastest.
Arguments:
- tiles: bfloat16 [8, 16, 128, 128, 128], P('row', 'col')
- tile_row: int32 [8, 16, 128], P('row', 'col'), may hold values from 0 to 15, as said below
- tile_col: int32 [8, 16, 128], P('row', 'col'), may hold values from 0 to 15
- tile_count: int32 [8, 16], P('row', 'col'), may hold values from 1 to 128, as said below
- sinogram: float32 [8, 2048, 128], P('row', 'col')
Outputs:
- volume: float32 [16, 2048, 128], P('col', 'row')
- residual: float32 [8, 2048, 128], P('row', 'col')
Inputs may be any that keep to these rules, and one draw needn't show every extreme that they name: Within one block the pairs (tile_row, tile_col) of all 128 slots are distinct. Slots 0 to tile_count - 1 of a block are live, the rest are ignored; some block has all 128 slots live in every draw.
All inputs are finite; a program needn't handle non-finite values.
Results may differ from a plain program's by a relative error of at most 0.015.
Values may be sent and summed in bfloat16 or wider, within the bound.
No kernel may reach another device: no remote copies, remote signals or barrier semaphores. Data moves between devices by JAX's collectives and lax.ppermute only.
A program may use at most 64 MiB of HBM per device.

v0:
```python
import functools

import jax
import jax.numpy as jnp
from jax import lax
from jax.experimental import pallas as pl
from jax.experimental.pallas import tpu as pltpu
from jax.sharding import Mesh
from jax.sharding import PartitionSpec as P


ROW = ("x", "k")
COL = ("y", "z")
NX, NK, NC = 4, 2, 16
TILE = 128
RAYS = 2048
VOX = 2048
FRAMES = 128
ITERS = 4
FH = FRAMES // NK
RS = RAYS // NC
RO = NK * RS
VS = VOX // NX
VH = VS // NK
VROWS = VS // 128 * FH
PAD = 8
LANES = 128
BF = jnp.bfloat16
F32 = jnp.float32


def vmem():
    return pl.BlockSpec(memory_space=pltpu.VMEM)


def smem():
    return pl.BlockSpec(memory_space=pltpu.SMEM)


def hbm():
    return pl.BlockSpec(memory_space=pltpu.HBM)


def shape(dims, dtype):
    return jax.ShapeDtypeStruct(dims, dtype)


def kernel(body, outs, ins, scratch=(), limit=4):
    return pl.pallas_call(
        body,
        out_shape=outs,
        in_specs=[smem() if a.dtype == jnp.int32 else vmem() for a in ins],
        out_specs=jax.tree.map(lambda _: vmem(), outs),
        scratch_shapes=list(scratch),
        compiler_params=pltpu.CompilerParams(vmem_limit_bytes=limit << 20),
    )(*ins)


def squares(values):
    total = values[:, :LANES] * values[:, :LANES]
    for i in range(LANES, values.shape[1], LANES):
        total += values[:, i : i + LANES] * values[:, i : i + LANES]
    square = jnp.concatenate([total, jnp.zeros((LANES - FH, LANES), F32)], axis=0)
    return jnp.sum(square.T, axis=0, keepdims=True)


def per_frame(row, width):
    column = jnp.broadcast_to(row, (LANES, LANES)).T[:FH]
    return jnp.concatenate([column] * (width // LANES), axis=1)


def as_rows(row):
    high = row.astype(BF).astype(F32)
    rest = row - high
    mid = rest.astype(BF).astype(F32)
    low = rest - mid
    i = lax.broadcasted_iota(jnp.int32, (PAD, LANES), 0)
    zero = jnp.zeros((PAD, LANES), F32)
    return jnp.where(i == 0, high, jnp.where(i == 1, mid, jnp.where(i == 2, low, zero))).astype(BF)


def row_of(rows):
    return jnp.sum(rows.astype(F32), axis=0, keepdims=True)


def wide(row):
    return jnp.broadcast_to(row, (8, LANES))


def stacked(values):
    return jnp.concatenate(
        [values[:, i : i + LANES] for i in range(0, values.shape[1], LANES)], axis=0
    )


def unstacked(rows):
    return jnp.concatenate([rows[i : i + FH] for i in range(0, rows.shape[0], FH)], axis=1)


def put(message, values, row):
    message[: message.shape[0] - PAD] = stacked(values.astype(BF))
    message[message.shape[0] - PAD :] = as_rows(row)


def put_all(message, values, row):
    part = stacked(values.astype(BF))
    rows = as_rows(row)
    for c in range(NC):
        message[c, : RO // LANES * FH] = part
        message[c, RO // LANES * FH :] = rows


def turn_body(k, sino, mine, other, turned):
    turned[...] = sino[...].T
    mine[...] = turned[pl.ds(pl.multiple_of(k[0] * FH, FH), FH)]
    other[...] = turned[pl.ds(pl.multiple_of((1 - k[0]) * FH, FH), FH)]


def start_body(mine, other, residual, message):
    values = jnp.concatenate([mine[...], other[...]], axis=1)
    residual[...] = values
    put_all(message, values, squares(values))


def build_body(x, table, table2, tiles, tiles2, after, dense, sem, sem2):
    shift = x[0] * (NC // NX)
    halves = ((table, tiles, sem), (table2, tiles2, sem2))

    def copy(half, t):
        index, stored, done = halves[half]
        r = pl.multiple_of(index[0, t] * TILE + half * RAYS, TILE)
        c = pl.multiple_of((index[1, t] + NC - shift) % NC * TILE, TILE)
        return pltpu.make_async_copy(stored.at[t], dense.at[pl.ds(r, TILE), pl.ds(c, TILE)], done)

    for half in range(NK):

        def start(t, carry, half=half):
            copy(half, t).start()
            return carry

        dense[half * RAYS : (half + 1) * RAYS] = jnp.zeros((RAYS, VOX), BF)
        lax.fori_loop(0, halves[half][0][2, 0], start, 0)
    for half in range(NK):

        def wait(t, carry, half=half):
            copy(half, t).wait()
            return carry

        lax.fori_loop(0, halves[half][0][2, 0], wait, 0)


def build(x, table, table2, tiles, tiles2, after):
    return pl.pallas_call(
        build_body,
        name="build",
        out_shape=pltpu.VMEM((NK * RAYS, VOX), BF),
        in_specs=[smem(), smem(), smem(), hbm(), hbm(), vmem()],
        out_specs=vmem(),
        scratch_shapes=[pltpu.SemaphoreType.DMA(()), pltpu.SemaphoreType.DMA(())],
        compiler_params=pltpu.CompilerParams(vmem_limit_bytes=44 << 20),
    )(x, table, table2, tiles, tiles2, after)


def turned_body(half, dense, turned):
    def turn(j, carry):
        voxels = pl.ds(pl.multiple_of(j * TILE, TILE), TILE)
        here = pl.ds(pl.multiple_of(j * TILE + half * VOX // 2, TILE), TILE)
        for i in range(0, NK * RAYS, TILE):
            turned[voxels, i : i + TILE] = dense[i : i + TILE, here].T
        return carry

    lax.fori_loop(0, VOX // 2 // TILE, turn, 0)


def turned_half(half, dense):
    return pl.pallas_call(
        functools.partial(turned_body, half),
        out_shape=pltpu.VMEM((VOX // 2, NK * RAYS), BF),
        in_specs=[vmem()],
        out_specs=vmem(),
        compiler_params=pltpu.CompilerParams(vmem_limit_bytes=4 << 20),
    )(dense)


def gather_body(arrived, dense, field, norm, far):
    seen = arrived[0, NK * FH :].astype(F32)
    for c in range(NC):
        for h in range(NK):
            field[:, h * RAYS + c * RS : h * RAYS + (c + 1) * RS] = arrived[c, h * FH : (h + 1) * FH]
        if c:
            seen += arrived[c, NK * FH :].astype(F32)
    row = row_of(seen)
    norm[...] = wide(row)
    part = jnp.dot(field[...], dense[:, 2 * VS : 3 * VS], preferred_element_type=F32)
    put(far, part, row)


def piece_body(j, field, norm, dense, out):
    part = jnp.dot(field[...], dense[:, j * VS : (j + 1) * VS], preferred_element_type=F32)
    if j:
        put(out, part, norm[0:1])
    else:
        out[...] = part


def arrived_sum(own, norm, pieces):
    value = own[...]
    row = norm[0:1]
    for p in pieces:
        value = value + unstacked(p[:VROWS].astype(F32))
        row = row + row_of(p[VROWS:])
    return value, row


def first_body(own, norm, p1, p2, p3, search, message, total):
    value, row = arrived_sum(own, norm, (p1, p2, p3))
    search[...] = value
    put(message, value, squares(value))
    total[...] = wide(row)


def next_body(first, own, norm, p1, p2, p3, *refs):
    if first:
        old, res, image, gamma, guess = refs[:5]
        outs = refs[5:]
    else:
        old, res, image, gamma, guess, beta, way, vol = refs[:8]
        outs = refs[8:]
    search, direction, volume, residual, message, step = outs
    value, row = arrived_sum(own, norm, (p1, p2, p3))
    alpha = gamma[0:1] / row
    ratio = per_frame(alpha / guess[0:1], VS)
    fresh = (1.0 - ratio) * old[...] + ratio * value
    search[...] = fresh
    put(message, fresh, squares(fresh))
    scale = per_frame(alpha, VS)
    if first:
        along = old[...]
        volume[...] = scale * along
    else:
        along = old[...] + per_frame(beta[0:1], VS) * way[...]
        volume[...] = vol[...] + scale * along
    direction[...] = along
    residual[...] = res[...] - scale[:, :RO] * image[...]
    step[...] = wide(alpha)


SIZE = 4 * RS


def part_of(places, messages, turned, at):
    total = None
    for j, m in zip(places, messages):
        part = jnp.dot(
            unstacked(m[:VROWS]),
            turned[j // 2][j % 2 * VS : (j % 2 + 1) * VS, at : at + SIZE],
            preferred_element_type=F32,
        )
        total = part if total is None else total + part
    return total


def here_body(here, turned0, image):
    for at in range(0, NK * RAYS, SIZE):
        image[:, at : at + SIZE] = part_of((0,), (here,), (turned0, None), at)


def far_body(far, turned1, so_far, image):
    for at in range(0, NK * RAYS, SIZE):
        part = part_of((2,), (far,), (None, turned1), at)
        image[:, at : at + SIZE] = so_far[:, at : at + SIZE] + part


def forward_body(near, back, turned0, turned1, so_far, here, far, out):
    row = jnp.zeros((1, LANES), F32)
    for m in (here, near, back, far):
        row = row + row_of(m[VROWS:])
    rows = as_rows(row)
    for c in range(NC):
        out[c, NK * FH :] = rows
    for at in range(0, NK * RAYS, SIZE):
        part = part_of((3, 1), (near, back), (turned0, turned1), at)
        part = (part + so_far[:, at : at + SIZE]).astype(BF)
        h, first = at // RAYS, at % RAYS // RS
        for c in range(SIZE // RS):
            out[first + c, h * FH : (h + 1) * FH] = part[:, c * RS : (c + 1) * RS]


def gathered(arrived):
    value = arrived[0].astype(F32)
    for c in range(1, NC):
        value = value + arrived[c].astype(F32)
    return unstacked(value[: NK * FH]), jnp.sum(value[NK * FH :], axis=0, keepdims=True)


def image_first_body(arrived, res, last, image, gamma, guess, message):
    value, row = gathered(arrived)
    image[...] = value
    gamma[...] = wide(row)
    about = last[0:1] / row
    about = jnp.where((about > 0.0) & (about < jnp.inf), about, 1.0)
    guess[...] = wide(about)
    put_all(message, res[...] - per_frame(about, RO) * value, squares(value))


def image_next_body(arrived, res, about, previous, last, image, gamma, beta, message):
    value, row = gathered(arrived)
    ratio = row / last[0:1]
    value = value + per_frame(ratio, RO) * previous[...]
    image[...] = value
    gamma[...] = wide(row)
    beta[...] = wide(ratio)
    put_all(message, res[...] - per_frame(about[0:1], RO) * value, squares(value))


def image_last_body(arrived, previous, last, image, gamma, beta, norms):
    value, row = gathered(arrived)
    ratio = row / last[0:1]
    value = value + per_frame(ratio, RO) * previous[...]
    image[...] = value
    gamma[...] = wide(row)
    beta[...] = wide(ratio)
    norm = wide(squares(value))
    for x in range(NX):
        norms[x] = norm


def norm_body(arrived, norms):
    total = arrived[0]
    for x in range(1, NX):
        total = total + arrived[x]
    for c in range(NC):
        norms[c] = total


def final_body(k, norms, gamma, search, beta, way, vol, res, image, mine, other, volume):
    total = norms[0, 0:1]
    for c in range(1, NC):
        total = total + norms[c, 0:1]
    alpha = per_frame(gamma[0:1] / total, VS)
    along = search[...] + per_frame(beta[0:1], VS) * way[...]
    volume[...] = vol[...] + alpha * along
    residual = res[...] - alpha[:, :RO] * image[...]
    mine[:, :VH] = volume[:, pl.ds(pl.multiple_of(k[0] * VH, VH), VH)]
    other[:, :VH] = volume[:, pl.ds(pl.multiple_of((1 - k[0]) * VH, VH), VH)]
    mine[:, VH:] = residual[:, :RS]
    other[:, VH:] = residual[:, RS:]


def finish_body(k, mine, other, volume, residual, turned):
    turned[pl.ds(pl.multiple_of(k[0] * FH, FH), FH)] = mine[...]
    turned[pl.ds(pl.multiple_of((1 - k[0]) * FH, FH), FH)] = other[...]
    whole = turned[...].T
    volume[...] = whole[:VH]
    residual[...] = whole[VH:]


def shifted(value, axis, by):
    n = lax.axis_size(axis)
    return lax.ppermute(value, axis, [(i, (i + by) % n) for i in range(n)])


def exchanged(parts, axis):
    return lax.all_to_all(parts, axis, split_axis=0, concat_axis=0, tiled=True)


LINE = (8, LANES)
COLUMN = (NC, NK * FH + PAD, RS)
SHARD = (VROWS + PAD, LANES)


def local(tiles, tile_row, tile_col, tile_count, sinogram):
    x = lax.axis_index("x").astype(jnp.int32).reshape(1)
    k = lax.axis_index("k").astype(jnp.int32).reshape(1)
    line = shape(LINE, F32)
    rays = shape((FH, RO), F32)
    voxels = shape((FH, VS), F32)
    column = shape(COLUMN, BF)
    shard = shape(SHARD, BF)

    table = jnp.concatenate(
        [tile_row[0], tile_col[0], jnp.broadcast_to(tile_count, tile_row.shape[1:])], axis=0
    )
    half = shape((FH, RS), F32)
    mine, other = kernel(
        turn_body, (half, half), (k, sinogram[0]), (pltpu.VMEM((FRAMES, RS), F32),)
    )
    table2 = shifted(table, "k", 1)
    other = shifted(other, "k", 1)
    stored, other, table2, x = lax.optimization_barrier((tiles[0, 0], other, table2, x))
    stored2 = shifted(stored, "k", 1)
    residual, message = kernel(start_body, (rays, column), (mine, other))
    arrived = exchanged(message, COL)
    dense = build(x, table, table2, stored, stored2, arrived)
    turned = (turned_half(0, dense), turned_half(1, dense))

    def backward_of(arrived):
        field, norm, p2 = kernel(
            gather_body, (shape((FH, NK * RAYS), BF), line, shard), (arrived, dense), limit=8
        )

        def piece(j, out):
            return kernel(functools.partial(piece_body, j), out, (field, norm, dense), limit=8)

        far = shifted(p2, "x", 2)
        p1 = piece(1, shard)
        near = shifted(p1, "x", 1)
        p3 = piece(3, shard)
        back = shifted(p3, "x", 3)
        return piece(0, voxels), norm, far, near, back

    def forward(message):
        far = shifted(message, "x", 2)
        near = shifted(message, "x", 1)
        back = shifted(message, "x", 3)
        whole = shape((FH, NK * RAYS), F32)
        image = kernel(here_body, whole, (message, turned[0]), limit=8)
        image = kernel(far_body, whole, (far, turned[1], image), limit=8)
        out = kernel(forward_body, column, (near, back, *turned, image, message, far), limit=8)
        return exchanged(out, COL)

    search, shard_out, last = kernel(first_body, (voxels, shard, line), backward_of(arrived))
    image, gamma, guess, message = kernel(
        image_first_body, (rays, line, line, column), (forward(shard_out), residual, last)
    )
    beta = direction = volume = None
    for step in range(1, ITERS):
        state = (search, residual, image, gamma, guess)
        if step > 1:
            state += (beta, direction, volume)

        def body(*refs, first=step == 1):
            next_body(first, *refs)

        search, direction, volume, residual, shard_out, guess = kernel(
            body,
            (voxels, voxels, voxels, rays, shard, line),
            (*backward_of(exchanged(message, COL)), *state),
        )
        arrived = forward(shard_out)
        if step + 1 < ITERS:
            image, gamma, beta, message = kernel(
                image_next_body,
                (rays, line, line, column),
                (arrived, residual, guess, image, gamma),
            )
    image, gamma, beta, norms = kernel(
        image_last_body, (rays, line, line, shape((NX, *LINE), F32)), (arrived, image, gamma)
    )
    norms = kernel(norm_body, shape((NC, *LINE), F32), (exchanged(norms, "x"),))
    both = shape((FH, VH + RS), F32)
    mine, other = kernel(
        final_body,
        (both, both),
        (k, exchanged(norms, COL), gamma, search, beta, direction, volume, residual, image),
        (pltpu.VMEM((FH, VS), F32),),
    )
    volume, residual = kernel(
        finish_body,
        (shape((VH, FRAMES), F32), shape((RS, FRAMES), F32)),
        (k, mine, shifted(other, "k", 1)),
        (pltpu.VMEM((FRAMES, VH + RS), F32),),
    )
    return volume[None], residual[None]


def solution(mesh):
    finer = Mesh(mesh.devices.reshape(4, 2, 4, 4), ("x", "k", "y", "z"))
    placed = (
        P(ROW, COL, None, None, None),
        P(ROW, COL, None),
        P(ROW, COL, None),
        P(ROW, COL),
        P(ROW, COL, None),
    )
    return jax.shard_map(
        local,
        mesh=finer,
        in_specs=placed,
        out_specs=(P(COL, ROW, None), P(ROW, COL, None)),
        check_vma=False,
    )
```

profile of v0, /device:TPU:0, one launch (start us, length us, event | category | flops | bytes accessed | tf_op | source)
XLA Modules:
  0.0 236.9 jit_solution(9852825456341806492)
XLA Ops:
  5.0 20.4 %all_to_all.50.after.arrived = bf16[16,136,128]{2,1,0:T(8,128)(2,1)} all-to-all(bf16[16,136,128]{2,1,0:T(8,128)(2,1)S(1)} %get-tuple-element.65), channel_id=1, replica_groups=mesh['x'=4,'k'=2,'y'=4,'z'=4] {'y','z'}, dimensions={0} | all-to-all | bytes 1114112 | tf_op jit(solution)/shard_map/all_to_all | solution.py:364
  25.4 4.7 %build.1.dense = bf16[4096,2048]{1,0:T(8,128)(2,1)S(1)} custom-call(s32[1]{0:T(128)} %bitcast.6.x, s32[3,128]{1,0:T(4,128)} %copy-done.2, s32[3,128]{1,0:T(4,128)} %copy-done.3, bf16[128,128,128]{2,1,0:T(8,128)(2,1)} %bitcast.14, bf16[128,128,128]{2,1,0:T(8,128)(2,1)} %collective-permute-done.2.tiles2, bf16[16,136,128]{2,1,0:T(8,128)(2,1)} %all_to_all.50.after.arrived), custom_call_target="tpu_custom_call" | custom-call | tf_op jit(solution)/shard_map/build/pallas_call | solution.py:153
  32.6 1.8 collective-permute-start.5
  34.7 2.0 collective-permute-start.3
  37.6 3.0 %collective-permute-done.4.p2 = bf16[264,128]{1,0:T(8,128)(2,1)S(1)} collective-permute-done((bf16[264,128]{1,0:T(8,128)(2,1)S(1)}, bf16[264,128]{1,0:T(8,128)(2,1)S(1)}, u32[]{:S(2)}, u32[]{:S(2)}) %collective-permute-start.4) | collective-permute-done | bytes 67616 | tf_op jit(solution)/shard_map/ppermute | solution.py:360
  40.8 2.0 collective-permute-start.8
  42.8 1.8 collective-permute-start.6
  44.5 1.5 collective-permute-start.7
  46.0 2.7 %shard_map.75.turned0 = bf16[1024,4096]{1,0:T(8,128)(2,1)S(1)} custom-call(bf16[4096,2048]{1,0:T(8,128)(2,1)S(1)} %build.1.dense), custom_call_target="tpu_custom_call" | custom-call | tf_op jit(solution)/shard_map/pallas_call | solution.py:176
  48.7 2.7 %shard_map.76.turned1 = bf16[1024,4096]{1,0:T(8,128)(2,1)S(1)} custom-call(bf16[4096,2048]{1,0:T(8,128)(2,1)S(1)} %build.1.dense), custom_call_target="tpu_custom_call" | custom-call | tf_op jit(solution)/shard_map/pallas_call | solution.py:176
  53.2 1.6 shard_map.79
  54.8 14.9 %all_to_all.51.arrived = bf16[16,136,128]{2,1,0:T(8,128)(2,1)S(1)} all-to-all(bf16[16,136,128]{2,1,0:T(8,128)(2,1)S(1)} %shard_map.79), channel_id=1, replica_groups=mesh['x'=4,'k'=2,'y'=4,'z'=4] {'y','z'}, dimensions={0} | all-to-all | bytes 1114112 | tf_op jit(solution)/shard_map/all_to_all | solution.py:364
  69.9 13.5 %all_to_all.52.arrived = bf16[16,136,128]{2,1,0:T(8,128)(2,1)S(1)} all-to-all(bf16[16,136,128]{2,1,0:T(8,128)(2,1)S(1)} %get-tuple-element.75), channel_id=1, replica_groups=mesh['x'=4,'k'=2,'y'=4,'z'=4] {'y','z'}, dimensions={0} | all-to-all | bytes 1114112 | tf_op jit(solution)/shard_map/all_to_all | solution.py:364
  83.4 0.9 shard_map.81
  86.1 2.0 collective-permute-start.10
  89.5 1.3 collective-permute-done.11.refs_4_
  90.8 1.9 collective-permute-done.10.refs_3_
  92.7 1.2 collective-permute-done.9.refs_2_
  94.1 1.0 collective-permute-start.14
  95.1 1.3 collective-permute-start.12
  96.3 2.0 collective-permute-start.13
  100.0 0.9 shard_map.87.so_far
  100.9 1.6 shard_map.88
  102.5 13.7 %all_to_all.53.arrived = bf16[16,136,128]{2,1,0:T(8,128)(2,1)S(1)} all-to-all(bf16[16,136,128]{2,1,0:T(8,128)(2,1)S(1)} %shard_map.88), channel_id=1, replica_groups=mesh['x'=4,'k'=2,'y'=4,'z'=4] {'y','z'}, dimensions={0} | all-to-all | bytes 1114112 | tf_op jit(solution)/shard_map/all_to_all | solution.py:364
  116.5 13.6 %all_to_all.54.arrived = bf16[16,136,128]{2,1,0:T(8,128)(2,1)S(1)} all-to-all(bf16[16,136,128]{2,1,0:T(8,128)(2,1)S(1)} %get-tuple-element.86), channel_id=1, replica_groups=mesh['x'=4,'k'=2,'y'=4,'z'=4] {'y','z'}, dimensions={0} | all-to-all | bytes 1114112 | tf_op jit(solution)/shard_map/all_to_all | solution.py:364
  130.1 0.9 shard_map.90
  132.7 4.5 %collective-permute-start.17 = (bf16[264,128]{1,0:T(8,128)(2,1)S(1)}, bf16[264,128]{1,0:T(8,128)(2,1)S(1)}, u32[]{:S(2)}, u32[]{:S(2)}) collective-permute-start(bf16[264,128]{1,0:T(8,128)(2,1)S(1)} %shard_map.93), channel_id=1, source_target_pairs={{0,96},{32,0},{64,32},{96,64},{1,97},{33,1},{65,33},{97,65},{2,98}... | collective-permute-start | bytes 202760 | tf_op jit(solution)/shard_map/ppermute | solution.py:360
  137.2 1.5 collective-permute-start.15
  139.6 3.8 %collective-permute-done.16.refs_3_ = bf16[264,128]{1,0:T(8,128)(2,1)S(1)} collective-permute-done((bf16[264,128]{1,0:T(8,128)(2,1)S(1)}, bf16[264,128]{1,0:T(8,128)(2,1)S(1)}, u32[]{:S(2)}, u32[]{:S(2)}) %collective-permute-start.16) | collective-permute-done | bytes 67616 | tf_op jit(solution)/shard_map/ppermute | solution.py:360
  143.7 1.2 collective-permute-start.20
  144.9 2.5 %collective-permute-start.18 = (bf16[264,128]{1,0:T(8,128)(2,1)S(1)}, bf16[264,128]{1,0:T(8,128)(2,1)S(1)}, u32[]{:S(2)}, u32[]{:S(2)}) collective-permute-start(bf16[264,128]{1,0:T(8,128)(2,1)S(1)} %get-tuple-element.96.here), channel_id=1, source_target_pairs={{0,32},{32,64},{64,96},{96,0},{1,33},{33,65},{65,97},{97,1},{2,34}... | collective-permute-start | bytes 202760 | tf_op jit(solution)/shard_map/ppermute | solution.py:360
  149.6 0.9 shard_map.96.so_far
  150.4 1.3 collective-permute-done.19.back
  151.7 1.6 shard_map.97
  153.3 13.5 %all_to_all.55.arrived = bf16[16,136,128]{2,1,0:T(8,128)(2,1)S(1)} all-to-all(bf16[16,136,128]{2,1,0:T(8,128)(2,1)S(1)} %shard_map.97), channel_id=1, replica_groups=mesh['x'=4,'k'=2,'y'=4,'z'=4] {'y','z'}, dimensions={0} | all-to-all | bytes 1114112 | tf_op jit(solution)/shard_map/all_to_all | solution.py:364
  167.1 13.5 %all_to_all.56.arrived = bf16[16,136,128]{2,1,0:T(8,128)(2,1)S(1)} all-to-all(bf16[16,136,128]{2,1,0:T(8,128)(2,1)S(1)} %get-tuple-element.99), channel_id=1, replica_groups=mesh['x'=4,'k'=2,'y'=4,'z'=4] {'y','z'}, dimensions={0} | all-to-all | bytes 1114112 | tf_op jit(solution)/shard_map/all_to_all | solution.py:364
  180.6 0.9 shard_map.99
  183.2 2.0 collective-permute-start.23
  185.3 1.4 collective-permute-start.21
  187.6 3.8 %collective-permute-done.22.refs_3_ = bf16[264,128]{1,0:T(8,128)(2,1)S(1)} collective-permute-done((bf16[264,128]{1,0:T(8,128)(2,1)S(1)}, bf16[264,128]{1,0:T(8,128)(2,1)S(1)}, u32[]{:S(2)}, u32[]{:S(2)}) %collective-permute-start.22) | collective-permute-done | bytes 67616 | tf_op jit(solution)/shard_map/ppermute | solution.py:360
  192.2 1.1 collective-permute-start.26
  193.3 2.5 %collective-permute-start.24 = (bf16[264,128]{1,0:T(8,128)(2,1)S(1)}, bf16[264,128]{1,0:T(8,128)(2,1)S(1)}, u32[]{:S(2)}, u32[]{:S(2)}) collective-permute-start(bf16[264,128]{1,0:T(8,128)(2,1)S(1)} %get-tuple-element.109.here), channel_id=1, source_target_pairs={{0,32},{32,64},{64,96},{96,0},{1,33},{33,65},{65,97},{97,1},{2,34}... | collective-permute-start | bytes 202760 | tf_op jit(solution)/shard_map/ppermute | solution.py:360
  198.8 1.3 collective-permute-done.25.back
  200.1 1.6 shard_map.106
  201.7 13.5 %all_to_all.57.arrived = bf16[16,136,128]{2,1,0:T(8,128)(2,1)S(1)} all-to-all(bf16[16,136,128]{2,1,0:T(8,128)(2,1)S(1)} %shard_map.106), channel_id=1, replica_groups=mesh['x'=4,'k'=2,'y'=4,'z'=4] {'y','z'}, dimensions={0} | all-to-all | bytes 1114112 | tf_op jit(solution)/shard_map/all_to_all | solution.py:364
  215.4 8.4 %all_to_all.58.arrived = f32[4,8,128]{2,1,0:T(8,128)S(1)} all-to-all(f32[4,8,128]{2,1,0:T(8,128)S(1)} %get-tuple-element.110), channel_id=1, replica_groups=mesh['x'=4,'k'=2,'y'=4,'z'=4] {'x'}, dimensions={0} | all-to-all | bytes 32768 | tf_op jit(solution)/shard_map/all_to_all | solution.py:364
  223.8 10.8 %all_to_all.59.norms = f32[16,8,128]{2,1,0:T(8,128)S(1)} all-to-all(f32[16,8,128]{2,1,0:T(8,128)S(1)} %shard_map.108), channel_id=1, replica_groups=mesh['x'=4,'k'=2,'y'=4,'z'=4] {'y','z'}, dimensions={0} | all-to-all | bytes 131072 | tf_op jit(solution)/shard_map/all_to_all | solution.py:364
  234.8 1.3 collective-permute-done.27.other
  (72 shorter events, 27.6 us)
Async XLA Ops:
  0.6 0.8 copy-start.1
  1.6 2.9 %collective-permute-start = (f32[64,128]{1,0:T(8,128)S(1)}, f32[64,128]{1,0:T(8,128)S(1)}, u32[]{:S(2)}, u32[]{:S(2)}) collective-permute-start(f32[64,128]{1,0:T(8,128)S(1)} %get-tuple-element.63), channel_id=1, source_target_pairs={{0,16},{16,0},{1,17},{17,1},{2,18},{18,2},{3,19},{19,3},{4,20},{20... | collective-permute-start | bytes 98312 | tf_op jit(solution)/shard_map/ppermute | solution.py:360
  3.1 22.2 %copy-start.2 = (s32[3,128]{1,0:T(4,128)}, s32[3,128]{1,0:T(4,128)S(1)}, u32[]{:S(2)}) copy-start(s32[3,128]{1,0:T(4,128)S(1)} %add_add_fusion.table) | copy-start | bytes 4612
  3.1 1.3 collective-permute-start.1
  4.5 20.9 %copy-start.3 = (s32[3,128]{1,0:T(4,128)}, s32[3,128]{1,0:T(4,128)S(1)}, u32[]{:S(2)}) copy-start(s32[3,128]{1,0:T(4,128)S(1)} %collective-permute-done.1.table2) | copy-start | bytes 4612
  4.5 20.9 %collective-permute-start.2 = (bf16[128,128,128]{2,1,0:T(8,128)(2,1)}, bf16[128,128,128]{2,1,0:T(8,128)(2,1)}, u32[]{:S(2)}, u32[]{:S(2)}) collective-permute-start(bf16[128,128,128]{2,1,0:T(8,128)(2,1)} %bitcast.13), channel_id=1, source_target_pairs={{0,16},{16,0},{1,17},{17,1},{2,18},{18,2},{3,19},{19,3},{4,20},{20... | collective-permute-start | bytes 12582920 | tf_op jit(solution)/shard_map/ppermute | solution.py:360
  25.4 4.7 %copy-start = (bf16[16,136,128]{2,1,0:T(8,128)(2,1)S(1)}, bf16[16,136,128]{2,1,0:T(8,128)(2,1)}, u32[]{:S(2)}) copy-start(bf16[16,136,128]{2,1,0:T(8,128)(2,1)} %all_to_all.50.after.arrived) | copy-start | bytes 1671172
  32.6 5.0 %collective-permute-start.5 = (bf16[264,128]{1,0:T(8,128)(2,1)S(1)}, bf16[264,128]{1,0:T(8,128)(2,1)S(1)}, u32[]{:S(2)}, u32[]{:S(2)}) collective-permute-start(bf16[264,128]{1,0:T(8,128)(2,1)S(1)} %shard_map.73), channel_id=1, source_target_pairs={{0,96},{32,0},{64,32},{96,64},{1,97},{33,1},{65,33},{97,65},{2,98}... | collective-permute-start | bytes 202760 | tf_op jit(solution)/shard_map/ppermute | solution.py:360
  34.4 6.2 %collective-permute-start.4 = (bf16[264,128]{1,0:T(8,128)(2,1)S(1)}, bf16[264,128]{1,0:T(8,128)(2,1)S(1)}, u32[]{:S(2)}, u32[]{:S(2)}) collective-permute-start(bf16[264,128]{1,0:T(8,128)(2,1)S(1)} %shard_map.72), channel_id=1, source_target_pairs={{0,32},{32,64},{64,96},{96,0},{1,33},{33,65},{65,97},{97,1},{2,34}... | collective-permute-start | bytes 202760 | tf_op jit(solution)/shard_map/ppermute | solution.py:360
  34.7 5.9 %collective-permute-start.3 = (bf16[264,128]{1,0:T(8,128)(2,1)S(1)}, bf16[264,128]{1,0:T(8,128)(2,1)S(1)}, u32[]{:S(2)}, u32[]{:S(2)}) collective-permute-start(bf16[264,128]{1,0:T(8,128)(2,1)S(1)} %get-tuple-element.71), channel_id=1, source_target_pairs={{0,64},{32,96},{64,0},{96,32},{1,65},{33,97},{65,1},{97,33},{2,66}... | collective-permute-start | bytes 202760 | tf_op jit(solution)/shard_map/ppermute | solution.py:360
  40.8 11.5 %collective-permute-start.8 = (bf16[264,128]{1,0:T(8,128)(2,1)S(1)}, bf16[264,128]{1,0:T(8,128)(2,1)S(1)}, u32[]{:S(2)}, u32[]{:S(2)}) collective-permute-start(bf16[264,128]{1,0:T(8,128)(2,1)S(1)} %get-tuple-element.72.here), channel_id=1, source_target_pairs={{0,64},{32,96},{64,0},{96,32},{1,65},{33,97},{65,1},{97,33},{2,66}... | collective-permute-start | bytes 202760 | tf_op jit(solution)/shard_map/ppermute | solution.py:360
  42.8 10.4 %collective-permute-start.6 = (bf16[264,128]{1,0:T(8,128)(2,1)S(1)}, bf16[264,128]{1,0:T(8,128)(2,1)S(1)}, u32[]{:S(2)}, u32[]{:S(2)}) collective-permute-start(bf16[264,128]{1,0:T(8,128)(2,1)S(1)} %get-tuple-element.72.here), channel_id=1, source_target_pairs={{0,32},{32,64},{64,96},{96,0},{1,33},{33,65},{65,97},{97,1},{2,34}... | collective-permute-start | bytes 202760 | tf_op jit(solution)/shard_map/ppermute | solution.py:360
  44.5 8.6 %collective-permute-start.7 = (bf16[264,128]{1,0:T(8,128)(2,1)S(1)}, bf16[264,128]{1,0:T(8,128)(2,1)S(1)}, u32[]{:S(2)}, u32[]{:S(2)}) collective-permute-start(bf16[264,128]{1,0:T(8,128)(2,1)S(1)} %get-tuple-element.72.here), channel_id=1, source_target_pairs={{0,96},{32,0},{64,32},{96,64},{1,97},{33,1},{65,33},{97,65},{2,98}... | collective-permute-start | bytes 202760 | tf_op jit(solution)/shard_map/ppermute | solution.py:360
  86.0 4.8 %collective-permute-start.11 = (bf16[264,128]{1,0:T(8,128)(2,1)S(1)}, bf16[264,128]{1,0:T(8,128)(2,1)S(1)}, u32[]{:S(2)}, u32[]{:S(2)}) collective-permute-start(bf16[264,128]{1,0:T(8,128)(2,1)S(1)} %shard_map.84), channel_id=1, source_target_pairs={{0,96},{32,0},{64,32},{96,64},{1,97},{33,1},{65,33},{97,65},{2,98}... | collective-permute-start | bytes 202760 | tf_op jit(solution)/shard_map/ppermute | solution.py:360
  86.1 6.5 %collective-permute-start.10 = (bf16[264,128]{1,0:T(8,128)(2,1)S(1)}, bf16[264,128]{1,0:T(8,128)(2,1)S(1)}, u32[]{:S(2)}, u32[]{:S(2)}) collective-permute-start(bf16[264,128]{1,0:T(8,128)(2,1)S(1)} %shard_map.83), channel_id=1, source_target_pairs={{0,32},{32,64},{64,96},{96,0},{1,33},{33,65},{65,97},{97,1},{2,34}... | collective-permute-start | bytes 202760 | tf_op jit(solution)/shard_map/ppermute | solution.py:360
  88.1 5.8 %collective-permute-start.9 = (bf16[264,128]{1,0:T(8,128)(2,1)S(1)}, bf16[264,128]{1,0:T(8,128)(2,1)S(1)}, u32[]{:S(2)}, u32[]{:S(2)}) collective-permute-start(bf16[264,128]{1,0:T(8,128)(2,1)S(1)} %get-tuple-element.78), channel_id=1, source_target_pairs={{0,64},{32,96},{64,0},{96,32},{1,65},{33,97},{65,1},{97,33},{2,66}... | collective-permute-start | bytes 202760 | tf_op jit(solution)/shard_map/ppermute | solution.py:360
  94.1 5.9 %collective-permute-start.14 = (bf16[264,128]{1,0:T(8,128)(2,1)S(1)}, bf16[264,128]{1,0:T(8,128)(2,1)S(1)}, u32[]{:S(2)}, u32[]{:S(2)}) collective-permute-start(bf16[264,128]{1,0:T(8,128)(2,1)S(1)} %get-tuple-element.83.here), channel_id=1, source_target_pairs={{0,64},{32,96},{64,0},{96,32},{1,65},{33,97},{65,1},{97,33},{2,66}... | collective-permute-start | bytes 202760 | tf_op jit(solution)/shard_map/ppermute | solution.py:360
  95.1 5.8 %collective-permute-start.12 = (bf16[264,128]{1,0:T(8,128)(2,1)S(1)}, bf16[264,128]{1,0:T(8,128)(2,1)S(1)}, u32[]{:S(2)}, u32[]{:S(2)}) collective-permute-start(bf16[264,128]{1,0:T(8,128)(2,1)S(1)} %get-tuple-element.83.here), channel_id=1, source_target_pairs={{0,32},{32,64},{64,96},{96,0},{1,33},{33,65},{65,97},{97,1},{2,34}... | collective-permute-start | bytes 202760 | tf_op jit(solution)/shard_map/ppermute | solution.py:360
  96.3 4.5 %collective-permute-start.13 = (bf16[264,128]{1,0:T(8,128)(2,1)S(1)}, bf16[264,128]{1,0:T(8,128)(2,1)S(1)}, u32[]{:S(2)}, u32[]{:S(2)}) collective-permute-start(bf16[264,128]{1,0:T(8,128)(2,1)S(1)} %get-tuple-element.83.here), channel_id=1, source_target_pairs={{0,96},{32,0},{64,32},{96,64},{1,97},{33,1},{65,33},{97,65},{2,98}... | collective-permute-start | bytes 202760 | tf_op jit(solution)/shard_map/ppermute | solution.py:360
  132.7 6.9 %collective-permute-start.17 = (bf16[264,128]{1,0:T(8,128)(2,1)S(1)}, bf16[264,128]{1,0:T(8,128)(2,1)S(1)}, u32[]{:S(2)}, u32[]{:S(2)}) collective-permute-start(bf16[264,128]{1,0:T(8,128)(2,1)S(1)} %shard_map.93), channel_id=1, source_target_pairs={{0,96},{32,0},{64,32},{96,64},{1,97},{33,1},{65,33},{97,65},{2,98}... | collective-permute-start | bytes 202760 | tf_op jit(solution)/shard_map/ppermute | solution.py:360
  137.2 6.2 %collective-permute-start.16 = (bf16[264,128]{1,0:T(8,128)(2,1)S(1)}, bf16[264,128]{1,0:T(8,128)(2,1)S(1)}, u32[]{:S(2)}, u32[]{:S(2)}) collective-permute-start(bf16[264,128]{1,0:T(8,128)(2,1)S(1)} %shard_map.92), channel_id=1, source_target_pairs={{0,32},{32,64},{64,96},{96,0},{1,33},{33,65},{65,97},{97,1},{2,34}... | collective-permute-start | bytes 202760 | tf_op jit(solution)/shard_map/ppermute | solution.py:360
  137.2 6.2 %collective-permute-start.15 = (bf16[264,128]{1,0:T(8,128)(2,1)S(1)}, bf16[264,128]{1,0:T(8,128)(2,1)S(1)}, u32[]{:S(2)}, u32[]{:S(2)}) collective-permute-start(bf16[264,128]{1,0:T(8,128)(2,1)S(1)} %get-tuple-element.89), channel_id=1, source_target_pairs={{0,64},{32,96},{64,0},{96,32},{1,65},{33,97},{65,1},{97,33},{2,66}... | collective-permute-start | bytes 202760 | tf_op jit(solution)/shard_map/ppermute | solution.py:360
  143.7 5.9 %collective-permute-start.20 = (bf16[264,128]{1,0:T(8,128)(2,1)S(1)}, bf16[264,128]{1,0:T(8,128)(2,1)S(1)}, u32[]{:S(2)}, u32[]{:S(2)}) collective-permute-start(bf16[264,128]{1,0:T(8,128)(2,1)S(1)} %get-tuple-element.96.here), channel_id=1, source_target_pairs={{0,64},{32,96},{64,0},{96,32},{1,65},{33,97},{65,1},{97,33},{2,66}... | collective-permute-start | bytes 202760 | tf_op jit(solution)/shard_map/ppermute | solution.py:360
  144.9 5.5 %collective-permute-start.18 = (bf16[264,128]{1,0:T(8,128)(2,1)S(1)}, bf16[264,128]{1,0:T(8,128)(2,1)S(1)}, u32[]{:S(2)}, u32[]{:S(2)}) collective-permute-start(bf16[264,128]{1,0:T(8,128)(2,1)S(1)} %get-tuple-element.96.here), channel_id=1, source_target_pairs={{0,32},{32,64},{64,96},{96,0},{1,33},{33,65},{65,97},{97,1},{2,34}... | collective-permute-start | bytes 202760 | tf_op jit(solution)/shard_map/ppermute | solution.py:360
  147.4 4.3 %collective-permute-start.19 = (bf16[264,128]{1,0:T(8,128)(2,1)S(1)}, bf16[264,128]{1,0:T(8,128)(2,1)S(1)}, u32[]{:S(2)}, u32[]{:S(2)}) collective-permute-start(bf16[264,128]{1,0:T(8,128)(2,1)S(1)} %get-tuple-element.96.here), channel_id=1, source_target_pairs={{0,96},{32,0},{64,32},{96,64},{1,97},{33,1},{65,33},{97,65},{2,98}... | collective-permute-start | bytes 202760 | tf_op jit(solution)/shard_map/ppermute | solution.py:360
  183.2 4.4 %collective-permute-start.23 = (bf16[264,128]{1,0:T(8,128)(2,1)S(1)}, bf16[264,128]{1,0:T(8,128)(2,1)S(1)}, u32[]{:S(2)}, u32[]{:S(2)}) collective-permute-start(bf16[264,128]{1,0:T(8,128)(2,1)S(1)} %shard_map.102), channel_id=1, source_target_pairs={{0,96},{32,0},{64,32},{96,64},{1,97},{33,1},{65,33},{97,65},{2,98}... | collective-permute-start | bytes 202760 | tf_op jit(solution)/shard_map/ppermute | solution.py:360
  185.2 6.2 %collective-permute-start.22 = (bf16[264,128]{1,0:T(8,128)(2,1)S(1)}, bf16[264,128]{1,0:T(8,128)(2,1)S(1)}, u32[]{:S(2)}, u32[]{:S(2)}) collective-permute-start(bf16[264,128]{1,0:T(8,128)(2,1)S(1)} %shard_map.101), channel_id=1, source_target_pairs={{0,32},{32,64},{64,96},{96,0},{1,33},{33,65},{65,97},{97,1},{2,34}... | collective-permute-start | bytes 202760 | tf_op jit(solution)/shard_map/ppermute | solution.py:360
  185.3 6.1 %collective-permute-start.21 = (bf16[264,128]{1,0:T(8,128)(2,1)S(1)}, bf16[264,128]{1,0:T(8,128)(2,1)S(1)}, u32[]{:S(2)}, u32[]{:S(2)}) collective-permute-start(bf16[264,128]{1,0:T(8,128)(2,1)S(1)} %get-tuple-element.102), channel_id=1, source_target_pairs={{0,64},{32,96},{64,0},{96,32},{1,65},{33,97},{65,1},{97,33},{2,66}... | collective-permute-start | bytes 202760 | tf_op jit(solution)/shard_map/ppermute | solution.py:360
  192.2 5.8 %collective-permute-start.26 = (bf16[264,128]{1,0:T(8,128)(2,1)S(1)}, bf16[264,128]{1,0:T(8,128)(2,1)S(1)}, u32[]{:S(2)}, u32[]{:S(2)}) collective-permute-start(bf16[264,128]{1,0:T(8,128)(2,1)S(1)} %get-tuple-element.109.here), channel_id=1, source_target_pairs={{0,64},{32,96},{64,0},{96,32},{1,65},{33,97},{65,1},{97,33},{2,66}... | collective-permute-start | bytes 202760 | tf_op jit(solution)/shard_map/ppermute | solution.py:360
  193.3 5.5 %collective-permute-start.24 = (bf16[264,128]{1,0:T(8,128)(2,1)S(1)}, bf16[264,128]{1,0:T(8,128)(2,1)S(1)}, u32[]{:S(2)}, u32[]{:S(2)}) collective-permute-start(bf16[264,128]{1,0:T(8,128)(2,1)S(1)} %get-tuple-element.109.here), channel_id=1, source_target_pairs={{0,32},{32,64},{64,96},{96,0},{1,33},{33,65},{65,97},{97,1},{2,34}... | collective-permute-start | bytes 202760 | tf_op jit(solution)/shard_map/ppermute | solution.py:360
  195.8 4.3 %collective-permute-start.25 = (bf16[264,128]{1,0:T(8,128)(2,1)S(1)}, bf16[264,128]{1,0:T(8,128)(2,1)S(1)}, u32[]{:S(2)}, u32[]{:S(2)}) collective-permute-start(bf16[264,128]{1,0:T(8,128)(2,1)S(1)} %get-tuple-element.109.here), channel_id=1, source_target_pairs={{0,96},{32,0},{64,32},{96,64},{1,97},{33,1},{65,33},{97,65},{2,98}... | collective-permute-start | bytes 202760 | tf_op jit(solution)/shard_map/ppermute | solution.py:360
  234.7 1.4 collective-permute-start.27
where the time goes:
time: 239 us; the launch traced here: 237 us
  blocking collectives  136 us (57%)
  Pallas kernels  40.3 us (17%)
  starting transfers between devices  35.5 us (15%)
  waiting for transfers between devices  21.8 us (9%)
    all_to_all x10, blocking collectives, exchanged(): return lax.all_to_all(parts, axis, split_axis=0, concat_axis=0, tiled=True)  136 us
    ppermute x28, starting transfers between devices, shifted(): return lax.ppermute(value, axis, [(i, (i + by) % n) for i in range(n)])  35.5 us
    pallas_call x41, Pallas kernels, kernel(): pl.pallas_call(body, out_shape=outs, in_specs=[smem() if a.dtype == jnp.i...  30.2 us
    ppermute x28, waiting for transfers between devices, shifted(): return lax.ppermute(value, axis, [(i, (i + by) % n) for i in range(n)])  21.8 us
    pallas_call x2, Pallas kernels, turned_half(): pl.pallas_call(functools.partial(turned_body, half), out_shape=pltpu.VMEM...  5.41 us
  transfers between devices with their start and end apart: 28, of which 13 were waited for; matrix products, arithmetic and copies ran while one was open for 0% of the time, Pallas kernels for 7%

commit v1 on v0

--- a/solution.py
+++ b/solution.py
@@ -110,16 +110,29 @@
         message[c, RO // LANES * FH :] = rows
 
 
-def turn_body(k, sino, mine, other, turned):
-    turned[...] = sino[...].T
+def turn_body(k, count, rows, cols, sino, mine, other, table, turned, rows_in, cols_in, sino_in, sems):
+    copies = [
+        pltpu.make_async_copy(source, target, sems.at[i])
+        for i, (source, target) in enumerate(((sino, sino_in), (rows, rows_in), (cols, cols_in)))
+    ]
+    for copy in copies:
+        copy.start()
+    for copy in copies:
+        copy.wait()
+    turned[...] = sino_in[...].T
     mine[...] = turned[pl.ds(pl.multiple_of(k[0] * FH, FH), FH)]
-    other[...] = turned[pl.ds(pl.multiple_of((1 - k[0]) * FH, FH), FH)]
-
-
-def start_body(mine, other, residual, message):
-    values = jnp.concatenate([mine[...], other[...]], axis=1)
+    other[:FH] = turned[pl.ds(pl.multiple_of((1 - k[0]) * FH, FH), FH)]
+    i = lax.broadcasted_iota(jnp.int32, (8, LANES), 0)
+    stored = jnp.where(i == 0, rows_in[...], jnp.where(i == 1, cols_in[...], count[0, 0]))
+    table[...] = stored
+    other[FH:] = stored.astype(F32)
+
+
+def start_body(mine, other, residual, message, table):
+    values = jnp.concatenate([mine[...], other[:FH]], axis=1)
     residual[...] = values
     put_all(message, values, squares(values))
+    table[...] = other[FH:].astype(jnp.int32)
 
 
 def build_body(x, table, table2, tiles, tiles2, after, dense, sem, sem2):
@@ -219,68 +232,60 @@
     total[...] = wide(row)
 
 
-def next_body(first, own, norm, p1, p2, p3, *refs):
-    if first:
-        old, res, image, gamma, guess = refs[:5]
-        outs = refs[5:]
-    else:
-        old, res, image, gamma, guess, beta, way, vol = refs[:8]
-        outs = refs[8:]
-    search, direction, volume, residual, message, step = outs
+def next_body(own, norm, p1, p2, p3, old, gamma, guess, search, message, step):
     value, row = arrived_sum(own, norm, (p1, p2, p3))
     alpha = gamma[0:1] / row
     ratio = per_frame(alpha / guess[0:1], VS)
     fresh = (1.0 - ratio) * old[...] + ratio * value
     search[...] = fresh
     put(message, fresh, squares(fresh))
-    scale = per_frame(alpha, VS)
+    step[...] = wide(alpha)
+
+
+def update_body(first, step, old, res, image, *refs):
+    direction, volume, residual = refs[-3:]
+    alpha = per_frame(step[0:1], VS)
     if first:
         along = old[...]
-        volume[...] = scale * along
+        volume[...] = alpha * along
     else:
+        beta, way, vol = refs[:3]
         along = old[...] + per_frame(beta[0:1], VS) * way[...]
-        volume[...] = vol[...] + scale * along
+        volume[...] = vol[...] + alpha * along
     direction[...] = along
-    residual[...] = res[...] - scale[:, :RO] * image[...]
-    step[...] = wide(alpha)
+    residual[...] = res[...] - alpha[:, :RO] * image[...]
 
 
 SIZE = 4 * RS
 
 
-def part_of(places, messages, turned, at):
-    total = None
-    for j, m in zip(places, messages):
-        part = jnp.dot(
-            unstacked(m[:VROWS]),
-            turned[j // 2][j % 2 * VS : (j % 2 + 1) * VS, at : at + SIZE],
-            preferred_element_type=F32,
-        )
-        total = part if total is None else total + part
-    return total
-
-
-def here_body(here, turned0, image):
+def part_of(j, message, turned, at):
+    first = j % 2 * VS
+    return jnp.dot(
+        unstacked(message[:VROWS]),
+        turned[first : first + VS, at : at + SIZE],
+        preferred_element_type=F32,
+    )
+
+
+def product_body(j, message, turned, *refs):
+    image = refs[-1]
     for at in range(0, NK * RAYS, SIZE):
-        image[:, at : at + SIZE] = part_of((0,), (here,), (turned0, None), at)
-
-
-def far_body(far, turned1, so_far, image):
-    for at in range(0, NK * RAYS, SIZE):
-        part = part_of((2,), (far,), (None, turned1), at)
-        image[:, at : at + SIZE] = so_far[:, at : at + SIZE] + part
-
-
-def forward_body(near, back, turned0, turned1, so_far, here, far, out):
+        part = part_of(j, message, turned, at)
+        if len(refs) > 1:
+            part = part + refs[0][:, at : at + SIZE]
+        image[:, at : at + SIZE] = part
+
+
+def forward_body(j, message, turned, so_far, m1, m2, m3, out):
     row = jnp.zeros((1, LANES), F32)
-    for m in (here, near, back, far):
+    for m in (message, m1, m2, m3):
         row = row + row_of(m[VROWS:])
     rows = as_rows(row)
     for c in range(NC):
         out[c, NK * FH :] = rows
     for at in range(0, NK * RAYS, SIZE):
-        part = part_of((3, 1), (near, back), (turned0, turned1), at)
-        part = (part + so_far[:, at : at + SIZE]).astype(BF)
+        part = (part_of(j, message, turned, at) + so_far[:, at : at + SIZE]).astype(BF)
         h, first = at // RAYS, at % RAYS // RS
         for c in range(SIZE // RS):
             out[first + c, h * FH : (h + 1) * FH] = part[:, c * RS : (c + 1) * RS]
@@ -313,22 +318,18 @@
     put_all(message, res[...] - per_frame(about[0:1], RO) * value, squares(value))
 
 
-def image_last_body(arrived, previous, last, image, gamma, beta, norms):
+def image_last_body(arrived, previous, last, image, gamma, beta, norm):
     value, row = gathered(arrived)
     ratio = row / last[0:1]
     value = value + per_frame(ratio, RO) * previous[...]
     image[...] = value
     gamma[...] = wide(row)
     beta[...] = wide(ratio)
-    norm = wide(squares(value))
-    for x in range(NX):
-        norms[x] = norm
-
-
-def norm_body(arrived, norms):
-    total = arrived[0]
-    for x in range(1, NX):
-        total = total + arrived[x]
+    norm[...] = wide(squares(value))
+
+
+def norm_body(mine, far, near, back, norms):
+    total = mine[...] + far[...] + near[...] + back[...]
     for c in range(NC):
         norms[c] = total
 
@@ -378,18 +379,28 @@
     column = shape(COLUMN, BF)
     shard = shape(SHARD, BF)
 
-    table = jnp.concatenate(
-        [tile_row[0], tile_col[0], jnp.broadcast_to(tile_count, tile_row.shape[1:])], axis=0
-    )
-    half = shape((FH, RS), F32)
-    mine, other = kernel(
-        turn_body, (half, half), (k, sinogram[0]), (pltpu.VMEM((FRAMES, RS), F32),)
-    )
-    table2 = shifted(table, "k", 1)
+    table_shape = shape((8, LANES), jnp.int32)
+    mine, other, table = pl.pallas_call(
+        turn_body,
+        name="turn",
+        out_shape=(shape((FH, RS), F32), shape((FH + 8, RS), F32), table_shape),
+        in_specs=[smem(), smem(), hbm(), hbm(), hbm()],
+        out_specs=(vmem(), vmem(), vmem()),
+        scratch_shapes=[
+            pltpu.VMEM((FRAMES, RS), F32),
+            pltpu.VMEM((1, LANES), jnp.int32),
+            pltpu.VMEM((1, LANES), jnp.int32),
+            pltpu.VMEM((RS, FRAMES), F32),
+            pltpu.SemaphoreType.DMA((3,)),
+        ],
+        compiler_params=pltpu.CompilerParams(vmem_limit_bytes=61 << 20),
+    )(k, tile_count, tile_row[0], tile_col[0], sinogram[0])
     other = shifted(other, "k", 1)
-    stored, other, table2, x = lax.optimization_barrier((tiles[0, 0], other, table2, x))
+    stored, other, x = lax.optimization_barrier((tiles[0, 0], other, x))
     stored2 = shifted(stored, "k", 1)
-    residual, message = kernel(start_body, (rays, column), (mine, other))
+    residual, message, table2 = kernel(
+        start_body, (rays, column, table_shape), (mine, other), limit=61
+    )
     arrived = exchanged(message, COL)
     dense = build(x, table, table2, stored, stored2, arrived)
     turned = (turned_half(0, dense), turned_half(1, dense))
@@ -409,45 +420,68 @@
         back = shifted(p3, "x", 3)
         return piece(0, voxels), norm, far, near, back
 
-    def forward(message):
+    def forward(message, update=None):
+        return forward_of(message, update)
+
+    def forward_of(message, update):
         far = shifted(message, "x", 2)
         near = shifted(message, "x", 1)
         back = shifted(message, "x", 3)
         whole = shape((FH, NK * RAYS), F32)
-        image = kernel(here_body, whole, (message, turned[0]), limit=8)
-        image = kernel(far_body, whole, (far, turned[1], image), limit=8)
-        out = kernel(forward_body, column, (near, back, *turned, image, message, far), limit=8)
-        return exchanged(out, COL)
+
+        def product(j, message, *so_far):
+            return kernel(
+                functools.partial(product_body, j),
+                whole,
+                (message, turned[j // 2], *so_far),
+                limit=8,
+            )
+
+        image = product(0, message)
+        updated = None
+        if update is not None:
+            updated = update()
+        image = product(3, near, image)
+        image = product(2, far, image)
+        out = kernel(
+            functools.partial(forward_body, 1),
+            column,
+            (back, turned[0], image, message, near, far),
+            limit=8,
+        )
+        return exchanged(out, COL), updated
 
     search, shard_out, last = kernel(first_body, (voxels, shard, line), backward_of(arrived))
     image, gamma, guess, message = kernel(
-        image_first_body, (rays, line, line, column), (forward(shard_out), residual, last)
+        image_first_body, (rays, line, line, column), (forward(shard_out)[0], residual, last)
     )
     beta = direction = volume = None
     for step in range(1, ITERS):
-        state = (search, residual, image, gamma, guess)
+        old = search
+        search, shard_out, guess = kernel(
+            next_body,
+            (voxels, shard, line),
+            (*backward_of(exchanged(message, COL)), old, gamma, guess),
+        )
+        state = (guess, old, residual, image)
         if step > 1:
             state += (beta, direction, volume)
 
-        def body(*refs, first=step == 1):
-            next_body(first, *refs)
-
-        search, direction, volume, residual, shard_out, guess = kernel(
-            body,
-            (voxels, voxels, voxels, rays, shard, line),
-            (*backward_of(exchanged(message, COL)), *state),
-        )
-        arrived = forward(shard_out)
+        def update(state=state, first=step == 1):
+            return kernel(functools.partial(update_body, first), (voxels, voxels, rays), state)
+
+        arrived, (direction, volume, residual) = forward(shard_out, update)
         if step + 1 < ITERS:
             image, gamma, beta, message = kernel(
                 image_next_body,
                 (rays, line, line, column),
                 (arrived, residual, guess, image, gamma),
             )
-    image, gamma, beta, norms = kernel(
-        image_last_body, (rays, line, line, shape((NX, *LINE), F32)), (arrived, image, gamma)
-    )
-    norms = kernel(norm_body, shape((NC, *LINE), F32), (exchanged(norms, "x"),))
+    image, gamma, beta, norm = kernel(
+        image_last_body, (rays, line, line, line), (arrived, image, gamma)
+    )
+    others = tuple(shifted(norm, "x", j) for j in (2, 1, 3))
+    norms = kernel(norm_body, shape((NC, *LINE), F32), (norm, *others))
     both = shape((FH, VH + RS), F32)
     mine, other = kernel(
         final_body,

time: 239 us -> 252 us (1.054)
  blocking collectives: 136 us -> 90.2 us
  waiting for transfers between devices: 21.8 us -> 48.5 us
  starting transfers between devices: 35.5 us -> 51.5 us
  local copies, waits for them, and re-layouts: 0.92 us -> 12 us
  Pallas kernels: 40.3 us -> 45.9 us
    all_to_all x10 -> x6, blocking collectives: 136 us -> 90.2 us  [exchanged(): return lax.all_to_all(parts, axis, split_axis=0, concat_axis=0, tiled=True)]
    all_to_all x0 -> x3, waiting for transfers between devices: none -> 28.1 us  [exchanged(): return lax.all_to_all(parts, axis, split_axis=0, concat_axis=0, tiled=True)]
    unnamed x8 -> x32, local copies, waits for them, and re-layouts: 0.84 us -> 12 us
    all_to_all x0 -> x3, starting transfers between devices: none -> 10.7 us  [exchanged(): return lax.all_to_all(parts, axis, split_axis=0, concat_axis=0, tiled=True)]
    ppermute x28 -> x30, starting transfers between devices: 35.5 us -> 40.8 us  [shifted(): return lax.ppermute(value, axis, [(i, (i + by) % n) for i in range(n)])]
    pallas_call x41 -> x47, Pallas kernels: 30.2 us -> 34.1 us  [kernel(): pl.pallas_call(body, out_shape=outs, in_specs=[smem() if a.dtype == jnp.i...]
    ppermute x28 -> x30, waiting for transfers between devices: 21.8 us -> 20.4 us  [shifted(): return lax.ppermute(value, axis, [(i, (i + by) % n) for i in range(n)])]
  transfers between devices with their start and end apart: 28 -> 33, of which waited for: 13 -> 19; matrix products, arithmetic and copies ran while one was open for 0% -> 0% of each run, Pallas kernels for 7% -> 8%
where the time goes in v1:
time: 252 us; the launch traced here: 250 us
  blocking collectives  90.2 us (36%)
  starting transfers between devices  51.5 us (20%)
  waiting for transfers between devices  48.5 us (19%)
  Pallas kernels  45.9 us (18%)
  local copies, waits for them, and re-layouts  12 us (5%)
    all_to_all x6, blocking collectives, exchanged(): return lax.all_to_all(parts, axis, split_axis=0, concat_axis=0, tiled=True)  90.2 us
    ppermute x30, starting transfers between devices, shifted(): return lax.ppermute(value, axis, [(i, (i + by) % n) for i in range(n)])  40.8 us
    pallas_call x47, Pallas kernels, kernel(): pl.pallas_call(body, out_shape=outs, in_specs=[smem() if a.dtype == jnp.i...  34.1 us
    all_to_all x3, waiting for transfers between devices, exchanged(): return lax.all_to_all(parts, axis, split_axis=0, concat_axis=0, tiled=True)  28.1 us
    ppermute x30, waiting for transfers between devices, shifted(): return lax.ppermute(value, axis, [(i, (i + by) % n) for i in range(n)])  20.4 us
    unnamed x32, local copies, waits for them, and re-layouts  12 us
    all_to_all x3, starting transfers between devices, exchanged(): return lax.all_to_all(parts, axis, split_axis=0, concat_axis=0, tiled=True)  10.7 us
    pallas_call x2, Pallas kernels, turned_half(): pl.pallas_call(functools.partial(turned_body, half), out_shape=pltpu.VMEM...  5.53 us
  transfers between devices with their start and end apart: 33, of which 19 were waited for; matrix products, arithmetic and copies ran while one was open for 0% of the time, Pallas kernels for 8%

profile of v1, /device:TPU:0, one launch (start us, length us, event | category | flops | bytes accessed | tf_op | source)
XLA Modules:
  0.0 250.0 jit_solution(13330495338090440193)
XLA Ops:
  1.3 1.6 turn.1
  3.0 1.4 collective-permute-done.other
  5.0 1.7 shard_map.68
  6.7 20.6 %all_to_all.45.after.arrived = bf16[16,136,128]{2,1,0:T(8,128)(2,1)} all-to-all(bf16[16,136,128]{2,1,0:T(8,128)(2,1)} %get-tuple-element.67), channel_id=1, replica_groups=mesh['x'=4,'k'=2,'y'=4,'z'=4] {'y','z'}, dimensions={0} | all-to-all | bytes 1114112 | tf_op jit(solution)/shard_map/all_to_all | solution.py:365
  27.3 4.7 %build.1.dense = bf16[4096,2048]{1,0:T(8,128)(2,1)S(1)} custom-call(s32[1]{0:T(128)} %bitcast.5.x, s32[8,128]{1,0:T(8,128)} %get-tuple-element.69.table, s32[8,128]{1,0:T(8,128)} %get-tuple-element.70.table2, bf16[128,128,128]{2,1,0:T(8,128)(2,1)} %bitcast.17, bf16[128,128,128]{2,1,0:T(8,128)(2,1)} %collective-permute-done.1.tiles2, ...), custom_call_target="tpu_custom_call" | custom-call | tf_op jit(solution)/shard_map/build/pallas_call | solution.py:166
  34.7 1.8 collective-permute-start.4
  36.8 2.0 collective-permute-start.2
  39.6 3.0 %collective-permute-done.3.p2 = bf16[264,128]{1,0:T(8,128)(2,1)S(1)} collective-permute-done((bf16[264,128]{1,0:T(8,128)(2,1)S(1)}, bf16[264,128]{1,0:T(8,128)(2,1)S(1)}, u32[]{:S(2)}, u32[]{:S(2)}) %collective-permute-start.3) | collective-permute-done | bytes 67616 | tf_op jit(solution)/shard_map/ppermute | solution.py:361
  43.6 3.5 %collective-permute-start.6 = (bf16[264,128]{1,0:T(8,128)(2,1)S(1)}, bf16[264,128]{1,0:T(8,128)(2,1)S(1)}, u32[]{:S(2)}, u32[]{:S(2)}) collective-permute-start(bf16[264,128]{1,0:T(8,128)(2,1)S(1)} %get-tuple-element.75.message.m1), channel_id=1, source_target_pairs={{0,64},{32,96},{64,0},{96,32},{1,65},{33,97},{65,1},{97,33},{2,66}... | collective-permute-start | bytes 202760 | tf_op jit(solution)/shard_map/ppermute | solution.py:361
  47.4 2.7 %shard_map.74.turned = bf16[1024,4096]{1,0:T(8,128)(2,1)S(1)} custom-call(bf16[4096,2048]{1,0:T(8,128)(2,1)S(1)} %build.1.dense), custom_call_target="tpu_custom_call" | custom-call | tf_op jit(solution)/shard_map/pallas_call | solution.py:189
  50.2 2.8 %shard_map.75.turned = bf16[1024,4096]{1,0:T(8,128)(2,1)S(1)} custom-call(bf16[4096,2048]{1,0:T(8,128)(2,1)S(1)} %build.1.dense), custom_call_target="tpu_custom_call" | custom-call | tf_op jit(solution)/shard_map/pallas_call | solution.py:189
  56.5 14.9 %all_to_all.46.arrived = bf16[16,136,128]{2,1,0:T(8,128)(2,1)S(1)} all-to-all(bf16[16,136,128]{2,1,0:T(8,128)(2,1)S(1)} %shard_map.79), channel_id=1, replica_groups=mesh['x'=4,'k'=2,'y'=4,'z'=4] {'y','z'}, dimensions={0} | all-to-all | bytes 1114112 | tf_op jit(solution)/shard_map/all_to_all | solution.py:365
  71.6 13.5 %all_to_all.47.arrived = bf16[16,136,128]{2,1,0:T(8,128)(2,1)S(1)} all-to-all(bf16[16,136,128]{2,1,0:T(8,128)(2,1)S(1)} %get-tuple-element.78), channel_id=1, replica_groups=mesh['x'=4,'k'=2,'y'=4,'z'=4] {'y','z'}, dimensions={0} | all-to-all | bytes 1114112 | tf_op jit(solution)/shard_map/all_to_all | solution.py:365
  88.2 1.8 collective-permute-start.9
  90.0 1.8 collective-permute-start.8
  92.6 1.4 collective-permute-done.9.p2
  94.0 1.8 collective-permute-done.8.p1
  96.0 1.8 collective-permute-start.13
  97.8 1.5 collective-permute-start.12
  99.3 1.3 collective-permute-start.11
  102.4 1.1 collective-permute-done.12.message.m3
  104.4 1.7 shard_map.89
  106.1 3.6 %all-to-all-start.3 = ((bf16[16,136,128]{2,1,0:T(8,128)(2,1)}), bf16[16,136,128]{2,1,0:T(8,128)(2,1)S(1)}, u32[]{:S(2)}, u32[]{:S(2)}) async-start(bf16[16,136,128]{2,1,0:T(8,128)(2,1)} %shard_map.89), calls=%async_computation.3 | async-start | bytes 1114112 | tf_op jit(solution)/shard_map/all_to_all | solution.py:365
  109.8 10.5 %all-to-all-done.3.arrived = bf16[16,136,128]{2,1,0:T(8,128)(2,1)S(1)} async-done(((bf16[16,136,128]{2,1,0:T(8,128)(2,1)}), bf16[16,136,128]{2,1,0:T(8,128)(2,1)S(1)}, u32[]{:S(2)}, u32[]{:S(2)}) %all-to-all-start.3) | async-done | bytes 557088 | tf_op jit(solution)/shard_map/all_to_all | solution.py:365
  120.5 14.0 %all_to_all.48.arrived = bf16[16,136,128]{2,1,0:T(8,128)(2,1)S(1)} all-to-all(bf16[16,136,128]{2,1,0:T(8,128)(2,1)S(1)} %get-tuple-element.89), channel_id=1, replica_groups=mesh['x'=4,'k'=2,'y'=4,'z'=4] {'y','z'}, dimensions={0} | all-to-all | bytes 1114112 | tf_op jit(solution)/shard_map/all_to_all | solution.py:365
  134.5 5.8 %copy-done.1 = bf16[4096,2048]{1,0:T(8,128)(2,1)S(1)} copy-done((bf16[4096,2048]{1,0:T(8,128)(2,1)S(1)}, bf16[4096,2048]{1,0:T(8,128)(2,1)}, u32[]{:S(2)}) %copy-start.1) | copy-done | bytes 16777240
  142.8 1.9 collective-permute-start.16
  144.9 1.4 collective-permute-start.14
  147.2 3.7 %collective-permute-done.15.p2 = bf16[264,128]{1,0:T(8,128)(2,1)S(1)} collective-permute-done((bf16[264,128]{1,0:T(8,128)(2,1)S(1)}, bf16[264,128]{1,0:T(8,128)(2,1)S(1)}, u32[]{:S(2)}, u32[]{:S(2)}) %collective-permute-start.15) | collective-permute-done | bytes 67616 | tf_op jit(solution)/shard_map/ppermute | solution.py:361
  151.4 4.1 %collective-permute-start.18 = (bf16[264,128]{1,0:T(8,128)(2,1)S(1)}, bf16[264,128]{1,0:T(8,128)(2,1)S(1)}, u32[]{:S(2)}, u32[]{:S(2)}) collective-permute-start(bf16[264,128]{1,0:T(8,128)(2,1)S(1)} %get-tuple-element.95.message.m1), channel_id=1, source_target_pairs={{0,64},{32,96},{64,0},{96,32},{1,65},{33,97},{65,1},{97,33},{2,66}... | collective-permute-start | bytes 202760 | tf_op jit(solution)/shard_map/ppermute | solution.py:361
  159.9 1.7 shard_map.100
  161.5 3.6 %all-to-all-start.5 = ((bf16[16,136,128]{2,1,0:T(8,128)(2,1)}), bf16[16,136,128]{2,1,0:T(8,128)(2,1)S(1)}, u32[]{:S(2)}, u32[]{:S(2)}) async-start(bf16[16,136,128]{2,1,0:T(8,128)(2,1)} %shard_map.100), calls=%async_computation.5 | async-start | bytes 1114112 | tf_op jit(solution)/shard_map/all_to_all | solution.py:365
  165.2 10.1 %all-to-all-done.5.arrived = bf16[16,136,128]{2,1,0:T(8,128)(2,1)S(1)} async-done(((bf16[16,136,128]{2,1,0:T(8,128)(2,1)}), bf16[16,136,128]{2,1,0:T(8,128)(2,1)S(1)}, u32[]{:S(2)}, u32[]{:S(2)}) %all-to-all-start.5) | async-done | bytes 557088 | tf_op jit(solution)/shard_map/all_to_all | solution.py:365
  175.6 13.7 %all_to_all.49.arrived = bf16[16,136,128]{2,1,0:T(8,128)(2,1)S(1)} all-to-all(bf16[16,136,128]{2,1,0:T(8,128)(2,1)S(1)} %get-tuple-element.102), channel_id=1, replica_groups=mesh['x'=4,'k'=2,'y'=4,'z'=4] {'y','z'}, dimensions={0} | all-to-all | bytes 1114112 | tf_op jit(solution)/shard_map/all_to_all | solution.py:365
  189.3 5.8 %copy-done.2 = bf16[4096,2048]{1,0:T(8,128)(2,1)S(1)} copy-done((bf16[4096,2048]{1,0:T(8,128)(2,1)S(1)}, bf16[4096,2048]{1,0:T(8,128)(2,1)}, u32[]{:S(2)}) %copy-start.2) | copy-done | bytes 16777240
  197.6 1.3 collective-permute-start.22
  199.7 2.5 collective-permute-start.20
  203.0 1.4 collective-permute-done.21.p2
  204.4 1.2 collective-permute-done.20.p1
  206.3 3.5 %collective-permute-start.24 = (bf16[264,128]{1,0:T(8,128)(2,1)S(1)}, bf16[264,128]{1,0:T(8,128)(2,1)S(1)}, u32[]{:S(2)}, u32[]{:S(2)}) collective-permute-start(bf16[264,128]{1,0:T(8,128)(2,1)S(1)} %get-tuple-element.108.message.m1), channel_id=1, source_target_pairs={{0,64},{32,96},{64,0},{96,32},{1,65},{33,97},{65,1},{97,33},{2,66}... | collective-permute-start | bytes 202760 | tf_op jit(solution)/shard_map/ppermute | solution.py:361
  209.8 1.1 collective-permute-start.23
  215.0 13.5 %all_to_all.50.arrived = bf16[16,136,128]{2,1,0:T(8,128)(2,1)S(1)} all-to-all(bf16[16,136,128]{2,1,0:T(8,128)(2,1)S(1)} %shard_map.111), channel_id=1, replica_groups=mesh['x'=4,'k'=2,'y'=4,'z'=4] {'y','z'}, dimensions={0} | all-to-all | bytes 1114112 | tf_op jit(solution)/shard_map/all_to_all | solution.py:365
  228.7 2.5 collective-permute-start.26
  231.9 2.5 collective-permute-start.28
  234.4 1.6 collective-permute-done.27.near
  236.6 3.5 %all-to-all-start.8 = ((f32[16,8,128]{2,1,0:T(8,128)}), f32[16,8,128]{2,1,0:T(8,128)S(1)}, u32[]{:S(2)}, u32[]{:S(2)}) async-start(f32[16,8,128]{2,1,0:T(8,128)} %shard_map.113), calls=%async_computation.8 | async-start | bytes 131072 | tf_op jit(solution)/shard_map/all_to_all | solution.py:365
  240.2 7.5 %all-to-all-done.8.norms = f32[16,8,128]{2,1,0:T(8,128)S(1)} async-done(((f32[16,8,128]{2,1,0:T(8,128)}), f32[16,8,128]{2,1,0:T(8,128)S(1)}, u32[]{:S(2)}, u32[]{:S(2)}) %all-to-all-start.8) | async-done | bytes 65568 | tf_op jit(solution)/shard_map/all_to_all | solution.py:365
  248.0 1.3 collective-permute-done.29.other
  (111 shorter events, 36.7 us)
Async XLA Ops:
  2.9 1.5 collective-permute-start
  4.4 22.9 %collective-permute-start.1 = (bf16[128,128,128]{2,1,0:T(8,128)(2,1)}, bf16[128,128,128]{2,1,0:T(8,128)(2,1)}, u32[]{:S(2)}, u32[]{:S(2)}) collective-permute-start(bf16[128,128,128]{2,1,0:T(8,128)(2,1)} %bitcast.16), channel_id=1, source_target_pairs={{0,16},{16,0},{1,17},{17,1},{2,18},{18,2},{3,19},{19,3},{4,20},{20... | collective-permute-start | bytes 12582920 | tf_op jit(solution)/shard_map/ppermute | solution.py:361
  27.3 4.7 %copy-start.5 = (bf16[16,136,128]{2,1,0:T(8,128)(2,1)S(1)}, bf16[16,136,128]{2,1,0:T(8,128)(2,1)}, u32[]{:S(2)}) copy-start(bf16[16,136,128]{2,1,0:T(8,128)(2,1)} %all_to_all.45.after.arrived) | copy-start | bytes 1671172
  32.0 59.7 %copy-start = (bf16[4096,2048]{1,0:T(8,128)(2,1)}, bf16[4096,2048]{1,0:T(8,128)(2,1)S(1)}, u32[]{:S(2)}) copy-start(bf16[4096,2048]{1,0:T(8,128)(2,1)S(1)} %build.1.dense) | copy-start | bytes 50331652
  34.7 5.0 %collective-permute-start.4 = (bf16[264,128]{1,0:T(8,128)(2,1)S(1)}, bf16[264,128]{1,0:T(8,128)(2,1)S(1)}, u32[]{:S(2)}, u32[]{:S(2)}) collective-permute-start(bf16[264,128]{1,0:T(8,128)(2,1)S(1)} %shard_map.72), channel_id=1, source_target_pairs={{0,96},{32,0},{64,32},{96,64},{1,97},{33,1},{65,33},{97,65},{2,98}... | collective-permute-start | bytes 202760 | tf_op jit(solution)/shard_map/ppermute | solution.py:361
  36.5 6.2 %collective-permute-start.3 = (bf16[264,128]{1,0:T(8,128)(2,1)S(1)}, bf16[264,128]{1,0:T(8,128)(2,1)S(1)}, u32[]{:S(2)}, u32[]{:S(2)}) collective-permute-start(bf16[264,128]{1,0:T(8,128)(2,1)S(1)} %shard_map.71), channel_id=1, source_target_pairs={{0,32},{32,64},{64,96},{96,0},{1,33},{33,65},{65,97},{97,1},{2,34}... | collective-permute-start | bytes 202760 | tf_op jit(solution)/shard_map/ppermute | solution.py:361
  36.8 5.9 %collective-permute-start.2 = (bf16[264,128]{1,0:T(8,128)(2,1)S(1)}, bf16[264,128]{1,0:T(8,128)(2,1)S(1)}, u32[]{:S(2)}, u32[]{:S(2)}) collective-permute-start(bf16[264,128]{1,0:T(8,128)(2,1)S(1)} %get-tuple-element.74), channel_id=1, source_target_pairs={{0,64},{32,96},{64,0},{96,32},{1,65},{33,97},{65,1},{97,33},{2,66}... | collective-permute-start | bytes 202760 | tf_op jit(solution)/shard_map/ppermute | solution.py:361
  42.8 11.0 %collective-permute-start.7 = (bf16[264,128]{1,0:T(8,128)(2,1)S(1)}, bf16[264,128]{1,0:T(8,128)(2,1)S(1)}, u32[]{:S(2)}, u32[]{:S(2)}) collective-permute-start(bf16[264,128]{1,0:T(8,128)(2,1)S(1)} %get-tuple-element.75.message.m1), channel_id=1, source_target_pairs={{0,32},{32,64},{64,96},{96,0},{1,33},{33,65},{65,97},{97,1},{2,34}... | collective-permute-start | bytes 202760 | tf_op jit(solution)/shard_map/ppermute | solution.py:361
  43.6 11.1 %collective-permute-start.6 = (bf16[264,128]{1,0:T(8,128)(2,1)S(1)}, bf16[264,128]{1,0:T(8,128)(2,1)S(1)}, u32[]{:S(2)}, u32[]{:S(2)}) collective-permute-start(bf16[264,128]{1,0:T(8,128)(2,1)S(1)} %get-tuple-element.75.message.m1), channel_id=1, source_target_pairs={{0,64},{32,96},{64,0},{96,32},{1,65},{33,97},{65,1},{97,33},{2,66}... | collective-permute-start | bytes 202760 | tf_op jit(solution)/shard_map/ppermute | solution.py:361
  47.2 8.4 %collective-permute-start.5 = (bf16[264,128]{1,0:T(8,128)(2,1)S(1)}, bf16[264,128]{1,0:T(8,128)(2,1)S(1)}, u32[]{:S(2)}, u32[]{:S(2)}) collective-permute-start(bf16[264,128]{1,0:T(8,128)(2,1)S(1)} %get-tuple-element.75.message.m1), channel_id=1, source_target_pairs={{0,96},{32,0},{64,32},{96,64},{1,97},{33,1},{65,33},{97,65},{2,98}... | collective-permute-start | bytes 202760 | tf_op jit(solution)/shard_map/ppermute | solution.py:361
  50.2 54.3 %copy-start.3 = (bf16[1024,4096]{1,0:T(8,128)(2,1)}, bf16[1024,4096]{1,0:T(8,128)(2,1)S(1)}, u32[]{:S(2)}) copy-start(bf16[1024,4096]{1,0:T(8,128)(2,1)S(1)} %shard_map.74.turned) | copy-start | bytes 25165828
  53.0 50.6 %copy-start.4 = (bf16[1024,4096]{1,0:T(8,128)(2,1)}, bf16[1024,4096]{1,0:T(8,128)(2,1)S(1)}, u32[]{:S(2)}) copy-start(bf16[1024,4096]{1,0:T(8,128)(2,1)S(1)} %shard_map.75.turned) | copy-start | bytes 25165828
  54.7 16.7 %copy-start.6 = (f32[64,256]{1,0:T(8,128)S(1)}, f32[64,256]{1,0:T(8,128)}, u32[]{:S(2)}) copy-start(f32[64,256]{1,0:T(8,128)} %get-tuple-element.76.res) | copy-start | bytes 196612
  87.7 4.9 %collective-permute-start.10 = (bf16[264,128]{1,0:T(8,128)(2,1)S(1)}, bf16[264,128]{1,0:T(8,128)(2,1)S(1)}, u32[]{:S(2)}, u32[]{:S(2)}) collective-permute-start(bf16[264,128]{1,0:T(8,128)(2,1)S(1)} %shard_map.84), channel_id=1, source_target_pairs={{0,96},{32,0},{64,32},{96,64},{1,97},{33,1},{65,33},{97,65},{2,98}... | collective-permute-start | bytes 202760 | tf_op jit(solution)/shard_map/ppermute | solution.py:361
  88.2 5.8 %collective-permute-start.9 = (bf16[264,128]{1,0:T(8,128)(2,1)S(1)}, bf16[264,128]{1,0:T(8,128)(2,1)S(1)}, u32[]{:S(2)}, u32[]{:S(2)}) collective-permute-start(bf16[264,128]{1,0:T(8,128)(2,1)S(1)} %shard_map.83), channel_id=1, source_target_pairs={{0,32},{32,64},{64,96},{96,0},{1,33},{33,65},{65,97},{97,1},{2,34}... | collective-permute-start | bytes 202760 | tf_op jit(solution)/shard_map/ppermute | solution.py:361
  90.0 5.8 %collective-permute-start.8 = (bf16[264,128]{1,0:T(8,128)(2,1)S(1)}, bf16[264,128]{1,0:T(8,128)(2,1)S(1)}, u32[]{:S(2)}, u32[]{:S(2)}) collective-permute-start(bf16[264,128]{1,0:T(8,128)(2,1)S(1)} %get-tuple-element.81), channel_id=1, source_target_pairs={{0,64},{32,96},{64,0},{96,32},{1,65},{33,97},{65,1},{97,33},{2,66}... | collective-permute-start | bytes 202760 | tf_op jit(solution)/shard_map/ppermute | solution.py:361
  96.0 5.6 %collective-permute-start.13 = (bf16[264,128]{1,0:T(8,128)(2,1)S(1)}, bf16[264,128]{1,0:T(8,128)(2,1)S(1)}, u32[]{:S(2)}, u32[]{:S(2)}) collective-permute-start(bf16[264,128]{1,0:T(8,128)(2,1)S(1)} %get-tuple-element.85.message.m1), channel_id=1, source_target_pairs={{0,32},{32,64},{64,96},{96,0},{1,33},{33,65},{65,97},{97,1},{2,34}... | collective-permute-start | bytes 202760 | tf_op jit(solution)/shard_map/ppermute | solution.py:361
  97.8 5.8 %collective-permute-start.12 = (bf16[264,128]{1,0:T(8,128)(2,1)S(1)}, bf16[264,128]{1,0:T(8,128)(2,1)S(1)}, u32[]{:S(2)}, u32[]{:S(2)}) collective-permute-start(bf16[264,128]{1,0:T(8,128)(2,1)S(1)} %get-tuple-element.85.message.m1), channel_id=1, source_target_pairs={{0,64},{32,96},{64,0},{96,32},{1,65},{33,97},{65,1},{97,33},{2,66}... | collective-permute-start | bytes 202760 | tf_op jit(solution)/shard_map/ppermute | solution.py:361
  99.3 5.1 %collective-permute-start.11 = (bf16[264,128]{1,0:T(8,128)(2,1)S(1)}, bf16[264,128]{1,0:T(8,128)(2,1)S(1)}, u32[]{:S(2)}, u32[]{:S(2)}) collective-permute-start(bf16[264,128]{1,0:T(8,128)(2,1)S(1)} %get-tuple-element.85.message.m1), channel_id=1, source_target_pairs={{0,96},{32,0},{64,32},{96,64},{1,97},{33,1},{65,33},{97,65},{2,98}... | collective-permute-start | bytes 202760 | tf_op jit(solution)/shard_map/ppermute | solution.py:361
  106.1 14.1 %all-to-all-start.3 = ((bf16[16,136,128]{2,1,0:T(8,128)(2,1)}), bf16[16,136,128]{2,1,0:T(8,128)(2,1)S(1)}, u32[]{:S(2)}, u32[]{:S(2)}) async-start(bf16[16,136,128]{2,1,0:T(8,128)(2,1)} %shard_map.89), calls=%async_computation.3 | async-start | bytes 1114112 | tf_op jit(solution)/shard_map/all_to_all | solution.py:365
  134.5 5.8 %copy-start.1 = (bf16[4096,2048]{1,0:T(8,128)(2,1)S(1)}, bf16[4096,2048]{1,0:T(8,128)(2,1)}, u32[]{:S(2)}) copy-start(bf16[4096,2048]{1,0:T(8,128)(2,1)} %copy-done) | copy-start | bytes 50331652
  142.8 4.4 %collective-permute-start.16 = (bf16[264,128]{1,0:T(8,128)(2,1)S(1)}, bf16[264,128]{1,0:T(8,128)(2,1)S(1)}, u32[]{:S(2)}, u32[]{:S(2)}) collective-permute-start(bf16[264,128]{1,0:T(8,128)(2,1)S(1)} %shard_map.95), channel_id=1, source_target_pairs={{0,96},{32,0},{64,32},{96,64},{1,97},{33,1},{65,33},{97,65},{2,98}... | collective-permute-start | bytes 202760 | tf_op jit(solution)/shard_map/ppermute | solution.py:361
  144.7 6.2 %collective-permute-start.15 = (bf16[264,128]{1,0:T(8,128)(2,1)S(1)}, bf16[264,128]{1,0:T(8,128)(2,1)S(1)}, u32[]{:S(2)}, u32[]{:S(2)}) collective-permute-start(bf16[264,128]{1,0:T(8,128)(2,1)S(1)} %shard_map.94), channel_id=1, source_target_pairs={{0,32},{32,64},{64,96},{96,0},{1,33},{33,65},{65,97},{97,1},{2,34}... | collective-permute-start | bytes 202760 | tf_op jit(solution)/shard_map/ppermute | solution.py:361
  144.9 10.6 %slice-start = ((s8[8388608]{0:T(1024)(128)(4,1)}), s8[4194304]{0:T(1024)(128)(4,1)S(1)}, s32[]{:S(2)}) async-start(s8[8388608]{0:T(1024)(128)(4,1)} %bitcast.8), calls=%async_computation.9 | async-start | bytes 8388608
  144.9 11.8 %slice-start.4 = ((s8[8388608]{0:T(1024)(128)(4,1)}), s8[4194304]{0:T(1024)(128)(4,1)S(1)}, s32[]{:S(2)}) async-start(s8[8388608]{0:T(1024)(128)(4,1)} %bitcast.12), calls=%async_computation.13 | async-start | bytes 8388608
  144.9 10.6 %slice-start.1 = ((s8[8388608]{0:T(1024)(128)(4,1)}), s8[4194304]{0:T(1024)(128)(4,1)S(1)}, s32[]{:S(2)}) async-start(s8[8388608]{0:T(1024)(128)(4,1)} %bitcast.8), calls=%async_computation.10 | async-start | bytes 8388608
  144.9 11.8 %slice-start.5 = ((s8[8388608]{0:T(1024)(128)(4,1)}), s8[4194304]{0:T(1024)(128)(4,1)S(1)}, s32[]{:S(2)}) async-start(s8[8388608]{0:T(1024)(128)(4,1)} %bitcast.12), calls=%async_computation.14 | async-start | bytes 8388608
  144.9 6.0 %collective-permute-start.14 = (bf16[264,128]{1,0:T(8,128)(2,1)S(1)}, bf16[264,128]{1,0:T(8,128)(2,1)S(1)}, u32[]{:S(2)}, u32[]{:S(2)}) collective-permute-start(bf16[264,128]{1,0:T(8,128)(2,1)S(1)} %get-tuple-element.92), channel_id=1, source_target_pairs={{0,64},{32,96},{64,0},{96,32},{1,65},{33,97},{65,1},{97,33},{2,66}... | collective-permute-start | bytes 202760 | tf_op jit(solution)/shard_map/ppermute | solution.py:361
  151.1 5.6 %collective-permute-start.19 = (bf16[264,128]{1,0:T(8,128)(2,1)S(1)}, bf16[264,128]{1,0:T(8,128)(2,1)S(1)}, u32[]{:S(2)}, u32[]{:S(2)}) collective-permute-start(bf16[264,128]{1,0:T(8,128)(2,1)S(1)} %get-tuple-element.95.message.m1), channel_id=1, source_target_pairs={{0,32},{32,64},{64,96},{96,0},{1,33},{33,65},{65,97},{97,1},{2,34}... | collective-permute-start | bytes 202760 | tf_op jit(solution)/shard_map/ppermute | solution.py:361
  151.4 7.1 %collective-permute-start.18 = (bf16[264,128]{1,0:T(8,128)(2,1)S(1)}, bf16[264,128]{1,0:T(8,128)(2,1)S(1)}, u32[]{:S(2)}, u32[]{:S(2)}) collective-permute-start(bf16[264,128]{1,0:T(8,128)(2,1)S(1)} %get-tuple-element.95.message.m1), channel_id=1, source_target_pairs={{0,64},{32,96},{64,0},{96,32},{1,65},{33,97},{65,1},{97,33},{2,66}... | collective-permute-start | bytes 202760 | tf_op jit(solution)/shard_map/ppermute | solution.py:361
  155.6 4.3 %collective-permute-start.17 = (bf16[264,128]{1,0:T(8,128)(2,1)S(1)}, bf16[264,128]{1,0:T(8,128)(2,1)S(1)}, u32[]{:S(2)}, u32[]{:S(2)}) collective-permute-start(bf16[264,128]{1,0:T(8,128)(2,1)S(1)} %get-tuple-element.95.message.m1), channel_id=1, source_target_pairs={{0,96},{32,0},{64,32},{96,64},{1,97},{33,1},{65,33},{97,65},{2,98}... | collective-permute-start | bytes 202760 | tf_op jit(solution)/shard_map/ppermute | solution.py:361
  161.5 13.8 %all-to-all-start.5 = ((bf16[16,136,128]{2,1,0:T(8,128)(2,1)}), bf16[16,136,128]{2,1,0:T(8,128)(2,1)S(1)}, u32[]{:S(2)}, u32[]{:S(2)}) async-start(bf16[16,136,128]{2,1,0:T(8,128)(2,1)} %shard_map.100), calls=%async_computation.5 | async-start | bytes 1114112 | tf_op jit(solution)/shard_map/all_to_all | solution.py:365
  189.3 5.8 %copy-start.2 = (bf16[4096,2048]{1,0:T(8,128)(2,1)S(1)}, bf16[4096,2048]{1,0:T(8,128)(2,1)}, u32[]{:S(2)}) copy-start(bf16[4096,2048]{1,0:T(8,128)(2,1)} %copy-done) | copy-start | bytes 50331652
  197.6 5.4 %collective-permute-start.22 = (bf16[264,128]{1,0:T(8,128)(2,1)S(1)}, bf16[264,128]{1,0:T(8,128)(2,1)S(1)}, u32[]{:S(2)}, u32[]{:S(2)}) collective-permute-start(bf16[264,128]{1,0:T(8,128)(2,1)S(1)} %shard_map.106), channel_id=1, source_target_pairs={{0,96},{32,0},{64,32},{96,64},{1,97},{33,1},{65,33},{97,65},{2,98}... | collective-permute-start | bytes 202760 | tf_op jit(solution)/shard_map/ppermute | solution.py:361
  198.9 5.5 %collective-permute-start.21 = (bf16[264,128]{1,0:T(8,128)(2,1)S(1)}, bf16[264,128]{1,0:T(8,128)(2,1)S(1)}, u32[]{:S(2)}, u32[]{:S(2)}) collective-permute-start(bf16[264,128]{1,0:T(8,128)(2,1)S(1)} %shard_map.105), channel_id=1, source_target_pairs={{0,32},{32,64},{64,96},{96,0},{1,33},{33,65},{65,97},{97,1},{2,34}... | collective-permute-start | bytes 202760 | tf_op jit(solution)/shard_map/ppermute | solution.py:361
  199.7 11.2 %slice-start.2 = ((s8[8388608]{0:T(1024)(128)(4,1)}), s8[4194304]{0:T(1024)(128)(4,1)S(1)}, s32[]{:S(2)}) async-start(s8[8388608]{0:T(1024)(128)(4,1)} %bitcast.10), calls=%async_computation.11 | async-start | bytes 8388608
  199.7 12.0 %slice-start.6 = ((s8[8388608]{0:T(1024)(128)(4,1)}), s8[4194304]{0:T(1024)(128)(4,1)S(1)}, s32[]{:S(2)}) async-start(s8[8388608]{0:T(1024)(128)(4,1)} %bitcast.14), calls=%async_computation.15 | async-start | bytes 8388608
  199.7 11.2 %slice-start.3 = ((s8[8388608]{0:T(1024)(128)(4,1)}), s8[4194304]{0:T(1024)(128)(4,1)S(1)}, s32[]{:S(2)}) async-start(s8[8388608]{0:T(1024)(128)(4,1)} %bitcast.10), calls=%async_computation.12 | async-start | bytes 8388608
  199.7 12.0 %slice-start.7 = ((s8[8388608]{0:T(1024)(128)(4,1)}), s8[4194304]{0:T(1024)(128)(4,1)S(1)}, s32[]{:S(2)}) async-start(s8[8388608]{0:T(1024)(128)(4,1)} %bitcast.14), calls=%async_computation.16 | async-start | bytes 8388608
  199.7 5.9 %collective-permute-start.20 = (bf16[264,128]{1,0:T(8,128)(2,1)S(1)}, bf16[264,128]{1,0:T(8,128)(2,1)S(1)}, u32[]{:S(2)}, u32[]{:S(2)}) collective-permute-start(bf16[264,128]{1,0:T(8,128)(2,1)S(1)} %get-tuple-element.105), channel_id=1, source_target_pairs={{0,64},{32,96},{64,0},{96,32},{1,65},{33,97},{65,1},{97,33},{2,66}... | collective-permute-start | bytes 202760 | tf_op jit(solution)/shard_map/ppermute | solution.py:361
  205.8 5.9 %collective-permute-start.25 = (bf16[264,128]{1,0:T(8,128)(2,1)S(1)}, bf16[264,128]{1,0:T(8,128)(2,1)S(1)}, u32[]{:S(2)}, u32[]{:S(2)}) collective-permute-start(bf16[264,128]{1,0:T(8,128)(2,1)S(1)} %get-tuple-element.108.message.m1), channel_id=1, source_target_pairs={{0,32},{32,64},{64,96},{96,0},{1,33},{33,65},{65,97},{97,1},{2,34}... | collective-permute-start | bytes 202760 | tf_op jit(solution)/shard_map/ppermute | solution.py:361
  206.3 6.6 %collective-permute-start.24 = (bf16[264,128]{1,0:T(8,128)(2,1)S(1)}, bf16[264,128]{1,0:T(8,128)(2,1)S(1)}, u32[]{:S(2)}, u32[]{:S(2)}) collective-permute-start(bf16[264,128]{1,0:T(8,128)(2,1)S(1)} %get-tuple-element.108.message.m1), channel_id=1, source_target_pairs={{0,64},{32,96},{64,0},{96,32},{1,65},{33,97},{65,1},{97,33},{2,66}... | collective-permute-start | bytes 202760 | tf_op jit(solution)/shard_map/ppermute | solution.py:361
  209.8 4.3 %collective-permute-start.23 = (bf16[264,128]{1,0:T(8,128)(2,1)S(1)}, bf16[264,128]{1,0:T(8,128)(2,1)S(1)}, u32[]{:S(2)}, u32[]{:S(2)}) collective-permute-start(bf16[264,128]{1,0:T(8,128)(2,1)S(1)} %get-tuple-element.108.message.m1), channel_id=1, source_target_pairs={{0,96},{32,0},{64,32},{96,64},{1,97},{33,1},{65,33},{97,65},{2,98}... | collective-permute-start | bytes 202760 | tf_op jit(solution)/shard_map/ppermute | solution.py:361
  228.7 5.7 %collective-permute-start.26 = (f32[8,128]{1,0:T(8,128)S(1)}, f32[8,128]{1,0:T(8,128)S(1)}, u32[]{:S(2)}, u32[]{:S(2)}) collective-permute-start(f32[8,128]{1,0:T(8,128)S(1)} %get-tuple-element.110.mine), channel_id=1, source_target_pairs={{0,64},{32,96},{64,0},{96,32},{1,65},{33,97},{65,1},{97,33},{2,66}... | collective-permute-start | bytes 12296 | tf_op jit(solution)/shard_map/ppermute | solution.py:361
  231.2 4.8 %collective-permute-start.27 = (f32[8,128]{1,0:T(8,128)S(1)}, f32[8,128]{1,0:T(8,128)S(1)}, u32[]{:S(2)}, u32[]{:S(2)}) collective-permute-start(f32[8,128]{1,0:T(8,128)S(1)} %get-tuple-element.110.mine), channel_id=1, source_target_pairs={{0,32},{32,64},{64,96},{96,0},{1,33},{33,65},{65,97},{97,1},{2,34}... | collective-permute-start | bytes 12296 | tf_op jit(solution)/shard_map/ppermute | solution.py:361
  231.9 4.1 %collective-permute-start.28 = (f32[8,128]{1,0:T(8,128)S(1)}, f32[8,128]{1,0:T(8,128)S(1)}, u32[]{:S(2)}, u32[]{:S(2)}) collective-permute-start(f32[8,128]{1,0:T(8,128)S(1)} %get-tuple-element.110.mine), channel_id=1, source_target_pairs={{0,96},{32,0},{64,32},{96,64},{1,97},{33,1},{65,33},{97,65},{2,98}... | collective-permute-start | bytes 12296 | tf_op jit(solution)/shard_map/ppermute | solution.py:361
  236.6 11.1 %all-to-all-start.8 = ((f32[16,8,128]{2,1,0:T(8,128)}), f32[16,8,128]{2,1,0:T(8,128)S(1)}, u32[]{:S(2)}, u32[]{:S(2)}) async-start(f32[16,8,128]{2,1,0:T(8,128)} %shard_map.113), calls=%async_computation.8 | async-start | bytes 131072 | tf_op jit(solution)/shard_map/all_to_all | solution.py:365
  247.9 1.4 collective-permute-start.29
  (1 other events, 0.6 us)

commit v2 on v1

--- a/solution.py
+++ b/solution.py
@@ -110,39 +110,26 @@
         message[c, RO // LANES * FH :] = rows
 
 
-def turn_body(k, count, rows, cols, sino, mine, other, table, turned, rows_in, cols_in, sino_in, sems):
-    copies = [
-        pltpu.make_async_copy(source, target, sems.at[i])
-        for i, (source, target) in enumerate(((sino, sino_in), (rows, rows_in), (cols, cols_in)))
-    ]
-    for copy in copies:
-        copy.start()
-    for copy in copies:
-        copy.wait()
-    turned[...] = sino_in[...].T
+def turn_body(k, sino, mine, other, turned):
+    turned[...] = sino[...].T
     mine[...] = turned[pl.ds(pl.multiple_of(k[0] * FH, FH), FH)]
-    other[:FH] = turned[pl.ds(pl.multiple_of((1 - k[0]) * FH, FH), FH)]
-    i = lax.broadcasted_iota(jnp.int32, (8, LANES), 0)
-    stored = jnp.where(i == 0, rows_in[...], jnp.where(i == 1, cols_in[...], count[0, 0]))
-    table[...] = stored
-    other[FH:] = stored.astype(F32)
-
-
-def start_body(mine, other, residual, message, table):
-    values = jnp.concatenate([mine[...], other[:FH]], axis=1)
+    other[...] = turned[pl.ds(pl.multiple_of((1 - k[0]) * FH, FH), FH)]
+
+
+def start_body(mine, other, residual, message):
+    values = jnp.concatenate([mine[...], other[...]], axis=1)
     residual[...] = values
     put_all(message, values, squares(values))
-    table[...] = other[FH:].astype(jnp.int32)
 
 
 def build_body(x, table, table2, tiles, tiles2, after, dense, sem, sem2):
-    shift = x[0] * (NC // NX)
     halves = ((table, tiles, sem), (table2, tiles2, sem2))
 
     def copy(half, t):
         index, stored, done = halves[half]
         r = pl.multiple_of(index[0, t] * TILE + half * RAYS, TILE)
-        c = pl.multiple_of((index[1, t] + NC - shift) % NC * TILE, TILE)
+        piece = index[1, t] // (VS // TILE) ^ x[0]
+        c = pl.multiple_of(piece * VS + index[1, t] % (VS // TILE) * TILE, TILE)
         return pltpu.make_async_copy(stored.at[t], dense.at[pl.ds(r, TILE), pl.ds(c, TILE)], done)
 
     for half in range(NK):
@@ -356,9 +343,8 @@
     residual[...] = whole[VH:]
 
 
-def shifted(value, axis, by):
-    n = lax.axis_size(axis)
-    return lax.ppermute(value, axis, [(i, (i + by) % n) for i in range(n)])
+def swapped(value, axis, by):
+    return lax.ppermute(value, axis, [(i, i ^ by) for i in range(lax.axis_size(axis))])
 
 
 def exchanged(parts, axis):
@@ -379,28 +365,18 @@
     column = shape(COLUMN, BF)
     shard = shape(SHARD, BF)
 
-    table_shape = shape((8, LANES), jnp.int32)
-    mine, other, table = pl.pallas_call(
-        turn_body,
-        name="turn",
-        out_shape=(shape((FH, RS), F32), shape((FH + 8, RS), F32), table_shape),
-        in_specs=[smem(), smem(), hbm(), hbm(), hbm()],
-        out_specs=(vmem(), vmem(), vmem()),
-        scratch_shapes=[
-            pltpu.VMEM((FRAMES, RS), F32),
-            pltpu.VMEM((1, LANES), jnp.int32),
-            pltpu.VMEM((1, LANES), jnp.int32),
-            pltpu.VMEM((RS, FRAMES), F32),
-            pltpu.SemaphoreType.DMA((3,)),
-        ],
-        compiler_params=pltpu.CompilerParams(vmem_limit_bytes=61 << 20),
-    )(k, tile_count, tile_row[0], tile_col[0], sinogram[0])
-    other = shifted(other, "k", 1)
-    stored, other, x = lax.optimization_barrier((tiles[0, 0], other, x))
-    stored2 = shifted(stored, "k", 1)
-    residual, message, table2 = kernel(
-        start_body, (rays, column, table_shape), (mine, other), limit=61
-    )
+    table = jnp.concatenate(
+        [tile_row[0], tile_col[0], jnp.broadcast_to(tile_count, tile_row.shape[1:])], axis=0
+    )
+    half = shape((FH, RS), F32)
+    mine, other = kernel(
+        turn_body, (half, half), (k, sinogram[0]), (pltpu.VMEM((FRAMES, RS), F32),)
+    )
+    table2 = swapped(table, "k", 1)
+    other = swapped(other, "k", 1)
+    stored, other, table2, x = lax.optimization_barrier((tiles[0, 0], other, table2, x))
+    stored2 = swapped(stored, "k", 1)
+    residual, message = kernel(start_body, (rays, column), (mine, other))
     arrived = exchanged(message, COL)
     dense = build(x, table, table2, stored, stored2, arrived)
     turned = (turned_half(0, dense), turned_half(1, dense))
@@ -413,20 +389,20 @@
         def piece(j, out):
             return kernel(functools.partial(piece_body, j), out, (field, norm, dense), limit=8)
 
-        far = shifted(p2, "x", 2)
+        two = swapped(p2, "x", 2)
+        p3 = piece(3, shard)
+        three = swapped(p3, "x", 3)
         p1 = piece(1, shard)
-        near = shifted(p1, "x", 1)
-        p3 = piece(3, shard)
-        back = shifted(p3, "x", 3)
-        return piece(0, voxels), norm, far, near, back
+        one = swapped(p1, "x", 1)
+        return piece(0, voxels), norm, two, three, one
 
     def forward(message, update=None):
         return forward_of(message, update)
 
     def forward_of(message, update):
-        far = shifted(message, "x", 2)
-        near = shifted(message, "x", 1)
-        back = shifted(message, "x", 3)
+        two = swapped(message, "x", 2)
+        three = swapped(message, "x", 3)
+        one = swapped(message, "x", 1)
         whole = shape((FH, NK * RAYS), F32)
 
         def product(j, message, *so_far):
@@ -441,12 +417,12 @@
         updated = None
         if update is not None:
             updated = update()
-        image = product(3, near, image)
-        image = product(2, far, image)
+        image = product(2, two, image)
+        image = product(3, three, image)
         out = kernel(
             functools.partial(forward_body, 1),
             column,
-            (back, turned[0], image, message, near, far),
+            (one, turned[0], image, message, two, three),
             limit=8,
         )
         return exchanged(out, COL), updated
@@ -480,7 +456,7 @@
     image, gamma, beta, norm = kernel(
         image_last_body, (rays, line, line, line), (arrived, image, gamma)
     )
-    others = tuple(shifted(norm, "x", j) for j in (2, 1, 3))
+    others = tuple(swapped(norm, "x", j) for j in (2, 1, 3))
     norms = kernel(norm_body, shape((NC, *LINE), F32), (norm, *others))
     both = shape((FH, VH + RS), F32)
     mine, other = kernel(
@@ -492,7 +468,7 @@
     volume, residual = kernel(
         finish_body,
         (shape((VH, FRAMES), F32), shape((RS, FRAMES), F32)),
-        (k, mine, shifted(other, "k", 1)),
+        (k, mine, swapped(other, "k", 1)),
         (pltpu.VMEM((FRAMES, VH + RS), F32),),
     )
     return volume[None], residual[None]

time: 252 us -> 250 us (level)
  starting transfers between devices: 51.5 us -> 48.1 us
  waiting for transfers between devices: 48.5 us -> 51.8 us
  Pallas kernels: 45.9 us -> 42.9 us
    ppermute x30 -> x31, starting transfers between devices: 40.8 us -> 37.4 us  [swapped(): lax.ppermute(value, axis, [(i, i ^ by) for i in range(lax.axis_size(axis))])]
    ppermute x30 -> x31, waiting for transfers between devices: 20.4 us -> 23.7 us  [swapped(): lax.ppermute(value, axis, [(i, i ^ by) for i in range(lax.axis_size(axis))])]
    pallas_call x47 -> x48, Pallas kernels: 34.1 us -> 32.6 us  [kernel(): pl.pallas_call(body, out_shape=outs, in_specs=[smem() if a.dtype == jnp.i...]
    unnamed x32 -> x34, local copies, waits for them, and re-layouts: 12 us -> 12.4 us
  transfers between devices with their start and end apart: 33 -> 34, of which waited for: 19 -> 21; matrix products, arithmetic and copies ran while one was open for 0% -> 0% of each run, Pallas kernels for 8% -> 8%
where the time goes in v2:
time: 250 us; the launch traced here: 248 us
  blocking collectives  90.2 us (36%)
  waiting for transfers between devices  51.8 us (21%)
  starting transfers between devices  48.1 us (19%)
  Pallas kernels  42.9 us (17%)
  local copies, waits for them, and re-layouts  12.5 us (5%)
    all_to_all x6, blocking collectives, exchanged(): return lax.all_to_all(parts, axis, split_axis=0, concat_axis=0, tiled=True)  90.2 us
    ppermute x31, starting transfers between devices, swapped(): lax.ppermute(value, axis, [(i, i ^ by) for i in range(lax.axis_size(axis))])  37.4 us
    pallas_call x48, Pallas kernels, kernel(): pl.pallas_call(body, out_shape=outs, in_specs=[smem() if a.dtype == jnp.i...  32.6 us
    all_to_all x3, waiting for transfers between devices, exchanged(): return lax.all_to_all(parts, axis, split_axis=0, concat_axis=0, tiled=True)  28.1 us
    ppermute x31, waiting for transfers between devices, swapped(): lax.ppermute(value, axis, [(i, i ^ by) for i in range(lax.axis_size(axis))])  23.7 us
    unnamed x34, local copies, waits for them, and re-layouts  12.4 us
    all_to_all x3, starting transfers between devices, exchanged(): return lax.all_to_all(parts, axis, split_axis=0, concat_axis=0, tiled=True)  10.7 us
    pallas_call x2, Pallas kernels, turned_half(): pl.pallas_call(functools.partial(turned_body, half), out_shape=pltpu.VMEM...  5.53 us
  transfers between devices with their start and end apart: 34, of which 21 were waited for; matrix products, arithmetic and copies ran while one was open for 0% of the time, Pallas kernels for 8%

profile of v2, /device:TPU:0, one launch (start us, length us, event | category | flops | bytes accessed | tf_op | source)
XLA Modules:
  0.0 248.1 jit_solution(9273402507732472405)
XLA Ops:
  5.0 20.4 %all_to_all.45.after.arrived = bf16[16,136,128]{2,1,0:T(8,128)(2,1)} all-to-all(bf16[16,136,128]{2,1,0:T(8,128)(2,1)S(1)} %get-tuple-element.66), channel_id=1, replica_groups=mesh['x'=4,'k'=2,'y'=4,'z'=4] {'y','z'}, dimensions={0} | all-to-all | bytes 1114112 | tf_op jit(solution)/shard_map/all_to_all | solution.py:351
  25.4 4.8 %build.1.dense = bf16[4096,2048]{1,0:T(8,128)(2,1)S(1)} custom-call(s32[1]{0:T(128)} %bitcast.6.x, s32[3,128]{1,0:T(4,128)} %copy-done.7, s32[3,128]{1,0:T(4,128)} %copy-done.8, bf16[128,128,128]{2,1,0:T(8,128)(2,1)} %bitcast.22, bf16[128,128,128]{2,1,0:T(8,128)(2,1)} %collective-permute-done.2.tiles2, bf16[16,136,128]{2,1,0:T(8,128)(2,1)} %all_to_all.45.after.arrived), custom_call_target="tpu_custom_call" | custom-call | tf_op jit(solution)/shard_map/build/pallas_call | solution.py:153
  33.7 1.7 collective-permute-start.4
  35.4 1.6 collective-permute-start.3
  37.8 1.8 collective-permute-done.4.p2
  39.7 1.5 collective-permute-done.3.p1
  41.3 1.7 collective-permute-start.8
  43.0 1.6 collective-permute-start.7
  44.9 2.7 %shard_map.75.turned = bf16[1024,4096]{1,0:T(8,128)(2,1)S(1)} custom-call(bf16[4096,2048]{1,0:T(8,128)(2,1)S(1)} %build.1.dense), custom_call_target="tpu_custom_call" | custom-call | tf_op jit(solution)/shard_map/pallas_call | solution.py:176
  47.6 2.8 %shard_map.76.turned = bf16[1024,4096]{1,0:T(8,128)(2,1)S(1)} custom-call(bf16[4096,2048]{1,0:T(8,128)(2,1)S(1)} %build.1.dense), custom_call_target="tpu_custom_call" | custom-call | tf_op jit(solution)/shard_map/pallas_call | solution.py:176
  53.9 15.0 %all_to_all.46.arrived = bf16[16,136,128]{2,1,0:T(8,128)(2,1)S(1)} all-to-all(bf16[16,136,128]{2,1,0:T(8,128)(2,1)S(1)} %shard_map.80), channel_id=1, replica_groups=mesh['x'=4,'k'=2,'y'=4,'z'=4] {'y','z'}, dimensions={0} | all-to-all | bytes 1114112 | tf_op jit(solution)/shard_map/all_to_all | solution.py:351
  69.2 13.5 %all_to_all.47.arrived = bf16[16,136,128]{2,1,0:T(8,128)(2,1)S(1)} all-to-all(bf16[16,136,128]{2,1,0:T(8,128)(2,1)S(1)} %get-tuple-element.76), channel_id=1, replica_groups=mesh['x'=4,'k'=2,'y'=4,'z'=4] {'y','z'}, dimensions={0} | all-to-all | bytes 1114112 | tf_op jit(solution)/shard_map/all_to_all | solution.py:351
  85.3 1.9 collective-permute-start.11
  87.8 1.8 collective-permute-start.9
  90.5 2.3 collective-permute-done.10.p2
  92.8 1.0 collective-permute-done.9.p1
  94.0 1.7 collective-permute-start.14
  95.7 1.5 collective-permute-start.13
  98.4 1.5 collective-permute-done.14.message.m2
  102.1 1.7 shard_map.90
  103.8 3.6 %all-to-all-start.3 = ((bf16[16,136,128]{2,1,0:T(8,128)(2,1)}), bf16[16,136,128]{2,1,0:T(8,128)(2,1)S(1)}, u32[]{:S(2)}, u32[]{:S(2)}) async-start(bf16[16,136,128]{2,1,0:T(8,128)(2,1)} %shard_map.90), calls=%async_computation.3 | async-start | bytes 1114112 | tf_op jit(solution)/shard_map/all_to_all | solution.py:351
  107.5 10.5 %all-to-all-done.3.arrived = bf16[16,136,128]{2,1,0:T(8,128)(2,1)S(1)} async-done(((bf16[16,136,128]{2,1,0:T(8,128)(2,1)}), bf16[16,136,128]{2,1,0:T(8,128)(2,1)S(1)}, u32[]{:S(2)}, u32[]{:S(2)}) %all-to-all-start.3) | async-done | bytes 557088 | tf_op jit(solution)/shard_map/all_to_all | solution.py:351
  118.2 14.0 %all_to_all.48.arrived = bf16[16,136,128]{2,1,0:T(8,128)(2,1)S(1)} all-to-all(bf16[16,136,128]{2,1,0:T(8,128)(2,1)S(1)} %get-tuple-element.87), channel_id=1, replica_groups=mesh['x'=4,'k'=2,'y'=4,'z'=4] {'y','z'}, dimensions={0} | all-to-all | bytes 1114112 | tf_op jit(solution)/shard_map/all_to_all | solution.py:351
  132.2 5.8 %copy-done.1 = bf16[4096,2048]{1,0:T(8,128)(2,1)S(1)} copy-done((bf16[4096,2048]{1,0:T(8,128)(2,1)S(1)}, bf16[4096,2048]{1,0:T(8,128)(2,1)}, u32[]{:S(2)}) %copy-start.1) | copy-done | bytes 16777240
  141.0 1.6 collective-permute-start.16
  142.7 2.1 collective-permute-start.15
  146.5 2.0 collective-permute-done.15.p1
  148.8 2.1 collective-permute-start.20
  150.9 1.9 collective-permute-start.19
  153.6 1.0 collective-permute-done.20.message.m2
  157.3 1.7 shard_map.101
  158.9 3.6 %all-to-all-start.5 = ((bf16[16,136,128]{2,1,0:T(8,128)(2,1)}), bf16[16,136,128]{2,1,0:T(8,128)(2,1)S(1)}, u32[]{:S(2)}, u32[]{:S(2)}) async-start(bf16[16,136,128]{2,1,0:T(8,128)(2,1)} %shard_map.101), calls=%async_computation.5 | async-start | bytes 1114112 | tf_op jit(solution)/shard_map/all_to_all | solution.py:351
  162.6 10.1 %all-to-all-done.5.arrived = bf16[16,136,128]{2,1,0:T(8,128)(2,1)S(1)} async-done(((bf16[16,136,128]{2,1,0:T(8,128)(2,1)}), bf16[16,136,128]{2,1,0:T(8,128)(2,1)S(1)}, u32[]{:S(2)}, u32[]{:S(2)}) %all-to-all-start.5) | async-done | bytes 557088 | tf_op jit(solution)/shard_map/all_to_all | solution.py:351
  173.0 13.7 %all_to_all.49.arrived = bf16[16,136,128]{2,1,0:T(8,128)(2,1)S(1)} all-to-all(bf16[16,136,128]{2,1,0:T(8,128)(2,1)S(1)} %get-tuple-element.100), channel_id=1, replica_groups=mesh['x'=4,'k'=2,'y'=4,'z'=4] {'y','z'}, dimensions={0} | all-to-all | bytes 1114112 | tf_op jit(solution)/shard_map/all_to_all | solution.py:351
  186.7 5.8 %copy-done.2 = bf16[4096,2048]{1,0:T(8,128)(2,1)S(1)} copy-done((bf16[4096,2048]{1,0:T(8,128)(2,1)S(1)}, bf16[4096,2048]{1,0:T(8,128)(2,1)}, u32[]{:S(2)}) %copy-start.2) | copy-done | bytes 16777240
  195.6 1.5 collective-permute-start.22
  197.1 2.2 collective-permute-start.21
  201.1 1.9 collective-permute-done.21.p1
  203.2 2.2 collective-permute-start.26
  205.4 1.9 collective-permute-start.25
  212.6 13.5 %all_to_all.50.arrived = bf16[16,136,128]{2,1,0:T(8,128)(2,1)S(1)} all-to-all(bf16[16,136,128]{2,1,0:T(8,128)(2,1)S(1)} %shard_map.112), channel_id=1, replica_groups=mesh['x'=4,'k'=2,'y'=4,'z'=4] {'y','z'}, dimensions={0} | all-to-all | bytes 1114112 | tf_op jit(solution)/shard_map/all_to_all | solution.py:351
  226.3 1.4 collective-permute-start.27
  227.7 1.5 collective-permute-start.28
  229.2 1.3 collective-permute-start.29
  231.5 2.5 %collective-permute-done.29.back = f32[8,128]{1,0:T(8,128)S(1)} collective-permute-done((f32[8,128]{1,0:T(8,128)S(1)}, f32[8,128]{1,0:T(8,128)S(1)}, u32[]{:S(2)}, u32[]{:S(2)}) %collective-permute-start.29) | collective-permute-done | bytes 4128 | tf_op jit(solution)/shard_map/ppermute | solution.py:347
  234.7 3.5 %all-to-all-start.8 = ((f32[16,8,128]{2,1,0:T(8,128)}), f32[16,8,128]{2,1,0:T(8,128)S(1)}, u32[]{:S(2)}, u32[]{:S(2)}) async-start(f32[16,8,128]{2,1,0:T(8,128)} %shard_map.114), calls=%async_computation.8 | async-start | bytes 131072 | tf_op jit(solution)/shard_map/all_to_all | solution.py:351
  238.3 7.5 %all-to-all-done.8.norms = f32[16,8,128]{2,1,0:T(8,128)S(1)} async-done(((f32[16,8,128]{2,1,0:T(8,128)}), f32[16,8,128]{2,1,0:T(8,128)S(1)}, u32[]{:S(2)}, u32[]{:S(2)}) %all-to-all-start.8) | async-done | bytes 65568 | tf_op jit(solution)/shard_map/all_to_all | solution.py:351
  246.0 1.3 collective-permute-done.30.other
  (117 shorter events, 42.1 us)
Async XLA Ops:
  1.6 2.9 %collective-permute-start = (f32[64,128]{1,0:T(8,128)S(1)}, f32[64,128]{1,0:T(8,128)S(1)}, u32[]{:S(2)}, u32[]{:S(2)}) collective-permute-start(f32[64,128]{1,0:T(8,128)S(1)} %get-tuple-element.64), channel_id=1, source_target_pairs={{0,16},{16,0},{1,17},{17,1},{2,18},{18,2},{3,19},{19,3},{4,20},{20... | collective-permute-start | bytes 98312 | tf_op jit(solution)/shard_map/ppermute | solution.py:347
  3.1 22.2 %copy-start.7 = (s32[3,128]{1,0:T(4,128)}, s32[3,128]{1,0:T(4,128)S(1)}, u32[]{:S(2)}) copy-start(s32[3,128]{1,0:T(4,128)S(1)} %add_add_fusion.table) | copy-start | bytes 4612
  3.1 1.3 collective-permute-start.1
  4.5 20.9 %copy-start.8 = (s32[3,128]{1,0:T(4,128)}, s32[3,128]{1,0:T(4,128)S(1)}, u32[]{:S(2)}) copy-start(s32[3,128]{1,0:T(4,128)S(1)} %collective-permute-done.1.table2) | copy-start | bytes 4612
  4.5 20.9 %collective-permute-start.2 = (bf16[128,128,128]{2,1,0:T(8,128)(2,1)}, bf16[128,128,128]{2,1,0:T(8,128)(2,1)}, u32[]{:S(2)}, u32[]{:S(2)}) collective-permute-start(bf16[128,128,128]{2,1,0:T(8,128)(2,1)} %bitcast.21), channel_id=1, source_target_pairs={{0,16},{16,0},{1,17},{17,1},{2,18},{18,2},{3,19},{19,3},{4,20},{20... | collective-permute-start | bytes 12582920 | tf_op jit(solution)/shard_map/ppermute | solution.py:347
  30.2 59.4 %copy-start = (bf16[4096,2048]{1,0:T(8,128)(2,1)}, bf16[4096,2048]{1,0:T(8,128)(2,1)S(1)}, u32[]{:S(2)}) copy-start(bf16[4096,2048]{1,0:T(8,128)(2,1)S(1)} %build.1.dense) | copy-start | bytes 50331652
  32.8 5.0 %collective-permute-start.5 = (bf16[264,128]{1,0:T(8,128)(2,1)S(1)}, bf16[264,128]{1,0:T(8,128)(2,1)S(1)}, u32[]{:S(2)}, u32[]{:S(2)}) collective-permute-start(bf16[264,128]{1,0:T(8,128)(2,1)S(1)} %shard_map.73), channel_id=1, source_target_pairs={{0,32},{32,0},{64,96},{96,64},{1,33},{33,1},{65,97},{97,65},{2,34}... | collective-permute-start | bytes 202760 | tf_op jit(solution)/shard_map/ppermute | solution.py:347
  33.7 6.0 %collective-permute-start.4 = (bf16[264,128]{1,0:T(8,128)(2,1)S(1)}, bf16[264,128]{1,0:T(8,128)(2,1)S(1)}, u32[]{:S(2)}, u32[]{:S(2)}) collective-permute-start(bf16[264,128]{1,0:T(8,128)(2,1)S(1)} %shard_map.72), channel_id=1, source_target_pairs={{0,96},{32,64},{64,32},{96,0},{1,97},{33,65},{65,33},{97,1},{2,98}... | collective-permute-start | bytes 202760 | tf_op jit(solution)/shard_map/ppermute | solution.py:347
  35.4 5.8 %collective-permute-start.3 = (bf16[264,128]{1,0:T(8,128)(2,1)S(1)}, bf16[264,128]{1,0:T(8,128)(2,1)S(1)}, u32[]{:S(2)}, u32[]{:S(2)}) collective-permute-start(bf16[264,128]{1,0:T(8,128)(2,1)S(1)} %get-tuple-element.72), channel_id=1, source_target_pairs={{0,64},{32,96},{64,0},{96,32},{1,65},{33,97},{65,1},{97,33},{2,66}... | collective-permute-start | bytes 202760 | tf_op jit(solution)/shard_map/ppermute | solution.py:347
  41.3 10.0 %collective-permute-start.8 = (bf16[264,128]{1,0:T(8,128)(2,1)S(1)}, bf16[264,128]{1,0:T(8,128)(2,1)S(1)}, u32[]{:S(2)}, u32[]{:S(2)}) collective-permute-start(bf16[264,128]{1,0:T(8,128)(2,1)S(1)} %get-tuple-element.73.message.m1), channel_id=1, source_target_pairs={{0,64},{32,96},{64,0},{96,32},{1,65},{33,97},{65,1},{97,33},{2,66}... | collective-permute-start | bytes 202760 | tf_op jit(solution)/shard_map/ppermute | solution.py:347
  43.0 9.2 %collective-permute-start.7 = (bf16[264,128]{1,0:T(8,128)(2,1)S(1)}, bf16[264,128]{1,0:T(8,128)(2,1)S(1)}, u32[]{:S(2)}, u32[]{:S(2)}) collective-permute-start(bf16[264,128]{1,0:T(8,128)(2,1)S(1)} %get-tuple-element.73.message.m1), channel_id=1, source_target_pairs={{0,96},{32,64},{64,32},{96,0},{1,97},{33,65},{65,33},{97,1},{2,98}... | collective-permute-start | bytes 202760 | tf_op jit(solution)/shard_map/ppermute | solution.py:347
  44.6 8.4 %collective-permute-start.6 = (bf16[264,128]{1,0:T(8,128)(2,1)S(1)}, bf16[264,128]{1,0:T(8,128)(2,1)S(1)}, u32[]{:S(2)}, u32[]{:S(2)}) collective-permute-start(bf16[264,128]{1,0:T(8,128)(2,1)S(1)} %get-tuple-element.73.message.m1), channel_id=1, source_target_pairs={{0,32},{32,0},{64,96},{96,64},{1,33},{33,1},{65,97},{97,65},{2,34}... | collective-permute-start | bytes 202760 | tf_op jit(solution)/shard_map/ppermute | solution.py:347
  47.6 54.5 %copy-start.3 = (bf16[1024,4096]{1,0:T(8,128)(2,1)}, bf16[1024,4096]{1,0:T(8,128)(2,1)S(1)}, u32[]{:S(2)}) copy-start(bf16[1024,4096]{1,0:T(8,128)(2,1)S(1)} %shard_map.75.turned) | copy-start | bytes 25165828
  50.5 50.8 %copy-start.4 = (bf16[1024,4096]{1,0:T(8,128)(2,1)}, bf16[1024,4096]{1,0:T(8,128)(2,1)S(1)}, u32[]{:S(2)}) copy-start(bf16[1024,4096]{1,0:T(8,128)(2,1)S(1)} %shard_map.76.turned) | copy-start | bytes 25165828
  85.3 5.2 %collective-permute-start.11 = (bf16[264,128]{1,0:T(8,128)(2,1)S(1)}, bf16[264,128]{1,0:T(8,128)(2,1)S(1)}, u32[]{:S(2)}, u32[]{:S(2)}) collective-permute-start(bf16[264,128]{1,0:T(8,128)(2,1)S(1)} %shard_map.85), channel_id=1, source_target_pairs={{0,32},{32,0},{64,96},{96,64},{1,33},{33,1},{65,97},{97,65},{2,34}... | collective-permute-start | bytes 202760 | tf_op jit(solution)/shard_map/ppermute | solution.py:347
  87.2 5.5 %collective-permute-start.10 = (bf16[264,128]{1,0:T(8,128)(2,1)S(1)}, bf16[264,128]{1,0:T(8,128)(2,1)S(1)}, u32[]{:S(2)}, u32[]{:S(2)}) collective-permute-start(bf16[264,128]{1,0:T(8,128)(2,1)S(1)} %shard_map.84), channel_id=1, source_target_pairs={{0,96},{32,64},{64,32},{96,0},{1,97},{33,65},{65,33},{97,1},{2,98}... | collective-permute-start | bytes 202760 | tf_op jit(solution)/shard_map/ppermute | solution.py:347
  87.8 6.0 %collective-permute-start.9 = (bf16[264,128]{1,0:T(8,128)(2,1)S(1)}, bf16[264,128]{1,0:T(8,128)(2,1)S(1)}, u32[]{:S(2)}, u32[]{:S(2)}) collective-permute-start(bf16[264,128]{1,0:T(8,128)(2,1)S(1)} %get-tuple-element.79), channel_id=1, source_target_pairs={{0,64},{32,96},{64,0},{96,32},{1,65},{33,97},{65,1},{97,33},{2,66}... | collective-permute-start | bytes 202760 | tf_op jit(solution)/shard_map/ppermute | solution.py:347
  94.0 5.9 %collective-permute-start.14 = (bf16[264,128]{1,0:T(8,128)(2,1)S(1)}, bf16[264,128]{1,0:T(8,128)(2,1)S(1)}, u32[]{:S(2)}, u32[]{:S(2)}) collective-permute-start(bf16[264,128]{1,0:T(8,128)(2,1)S(1)} %get-tuple-element.83.message.m1), channel_id=1, source_target_pairs={{0,64},{32,96},{64,0},{96,32},{1,65},{33,97},{65,1},{97,33},{2,66}... | collective-permute-start | bytes 202760 | tf_op jit(solution)/shard_map/ppermute | solution.py:347
  95.7 5.5 %collective-permute-start.13 = (bf16[264,128]{1,0:T(8,128)(2,1)S(1)}, bf16[264,128]{1,0:T(8,128)(2,1)S(1)}, u32[]{:S(2)}, u32[]{:S(2)}) collective-permute-start(bf16[264,128]{1,0:T(8,128)(2,1)S(1)} %get-tuple-element.83.message.m1), channel_id=1, source_target_pairs={{0,96},{32,64},{64,32},{96,0},{1,97},{33,65},{65,33},{97,1},{2,98}... | collective-permute-start | bytes 202760 | tf_op jit(solution)/shard_map/ppermute | solution.py:347
  97.2 4.9 %collective-permute-start.12 = (bf16[264,128]{1,0:T(8,128)(2,1)S(1)}, bf16[264,128]{1,0:T(8,128)(2,1)S(1)}, u32[]{:S(2)}, u32[]{:S(2)}) collective-permute-start(bf16[264,128]{1,0:T(8,128)(2,1)S(1)} %get-tuple-element.83.message.m1), channel_id=1, source_target_pairs={{0,32},{32,0},{64,96},{96,64},{1,33},{33,1},{65,97},{97,65},{2,34}... | collective-permute-start | bytes 202760 | tf_op jit(solution)/shard_map/ppermute | solution.py:347
  103.8 14.1 %all-to-all-start.3 = ((bf16[16,136,128]{2,1,0:T(8,128)(2,1)}), bf16[16,136,128]{2,1,0:T(8,128)(2,1)S(1)}, u32[]{:S(2)}, u32[]{:S(2)}) async-start(bf16[16,136,128]{2,1,0:T(8,128)(2,1)} %shard_map.90), calls=%async_computation.3 | async-start | bytes 1114112 | tf_op jit(solution)/shard_map/all_to_all | solution.py:351
  132.2 5.8 %copy-start.1 = (bf16[4096,2048]{1,0:T(8,128)(2,1)S(1)}, bf16[4096,2048]{1,0:T(8,128)(2,1)}, u32[]{:S(2)}) copy-start(bf16[4096,2048]{1,0:T(8,128)(2,1)} %copy-done) | copy-start | bytes 50331652
  140.5 5.1 %collective-permute-start.17 = (bf16[264,128]{1,0:T(8,128)(2,1)S(1)}, bf16[264,128]{1,0:T(8,128)(2,1)S(1)}, u32[]{:S(2)}, u32[]{:S(2)}) collective-permute-start(bf16[264,128]{1,0:T(8,128)(2,1)S(1)} %shard_map.96), channel_id=1, source_target_pairs={{0,32},{32,0},{64,96},{96,64},{1,33},{33,1},{65,97},{97,65},{2,34}... | collective-permute-start | bytes 202760 | tf_op jit(solution)/shard_map/ppermute | solution.py:347
  141.0 5.5 %collective-permute-start.16 = (bf16[264,128]{1,0:T(8,128)(2,1)S(1)}, bf16[264,128]{1,0:T(8,128)(2,1)S(1)}, u32[]{:S(2)}, u32[]{:S(2)}) collective-permute-start(bf16[264,128]{1,0:T(8,128)(2,1)S(1)} %shard_map.95), channel_id=1, source_target_pairs={{0,96},{32,64},{64,32},{96,0},{1,97},{33,65},{65,33},{97,1},{2,98}... | collective-permute-start | bytes 202760 | tf_op jit(solution)/shard_map/ppermute | solution.py:347
  142.7 10.1 %slice-start = ((s8[8388608]{0:T(1024)(128)(4,1)}), s8[4194304]{0:T(1024)(128)(4,1)S(1)}, s32[]{:S(2)}) async-start(s8[8388608]{0:T(1024)(128)(4,1)} %bitcast.12), calls=%async_computation.9 | async-start | bytes 8388608
  142.7 12.0 %slice-start.4 = ((s8[8388608]{0:T(1024)(128)(4,1)}), s8[4194304]{0:T(1024)(128)(4,1)S(1)}, s32[]{:S(2)}) async-start(s8[8388608]{0:T(1024)(128)(4,1)} %bitcast.16), calls=%async_computation.13 | async-start | bytes 8388608
  142.7 10.1 %slice-start.1 = ((s8[8388608]{0:T(1024)(128)(4,1)}), s8[4194304]{0:T(1024)(128)(4,1)S(1)}, s32[]{:S(2)}) async-start(s8[8388608]{0:T(1024)(128)(4,1)} %bitcast.12), calls=%async_computation.10 | async-start | bytes 8388608
  142.7 12.0 %slice-start.5 = ((s8[8388608]{0:T(1024)(128)(4,1)}), s8[4194304]{0:T(1024)(128)(4,1)S(1)}, s32[]{:S(2)}) async-start(s8[8388608]{0:T(1024)(128)(4,1)} %bitcast.16), calls=%async_computation.14 | async-start | bytes 8388608
  142.7 5.9 %collective-permute-start.15 = (bf16[264,128]{1,0:T(8,128)(2,1)S(1)}, bf16[264,128]{1,0:T(8,128)(2,1)S(1)}, u32[]{:S(2)}, u32[]{:S(2)}) collective-permute-start(bf16[264,128]{1,0:T(8,128)(2,1)S(1)} %get-tuple-element.90), channel_id=1, source_target_pairs={{0,64},{32,96},{64,0},{96,32},{1,65},{33,97},{65,1},{97,33},{2,66}... | collective-permute-start | bytes 202760 | tf_op jit(solution)/shard_map/ppermute | solution.py:347
  148.8 5.9 %collective-permute-start.20 = (bf16[264,128]{1,0:T(8,128)(2,1)S(1)}, bf16[264,128]{1,0:T(8,128)(2,1)S(1)}, u32[]{:S(2)}, u32[]{:S(2)}) collective-permute-start(bf16[264,128]{1,0:T(8,128)(2,1)S(1)} %get-tuple-element.93.message.m1), channel_id=1, source_target_pairs={{0,64},{32,96},{64,0},{96,32},{1,65},{33,97},{65,1},{97,33},{2,66}... | collective-permute-start | bytes 202760 | tf_op jit(solution)/shard_map/ppermute | solution.py:347
  150.9 5.5 %collective-permute-start.19 = (bf16[264,128]{1,0:T(8,128)(2,1)S(1)}, bf16[264,128]{1,0:T(8,128)(2,1)S(1)}, u32[]{:S(2)}, u32[]{:S(2)}) collective-permute-start(bf16[264,128]{1,0:T(8,128)(2,1)S(1)} %get-tuple-element.93.message.m1), channel_id=1, source_target_pairs={{0,96},{32,64},{64,32},{96,0},{1,97},{33,65},{65,33},{97,1},{2,98}... | collective-permute-start | bytes 202760 | tf_op jit(solution)/shard_map/ppermute | solution.py:347
  152.8 4.5 %collective-permute-start.18 = (bf16[264,128]{1,0:T(8,128)(2,1)S(1)}, bf16[264,128]{1,0:T(8,128)(2,1)S(1)}, u32[]{:S(2)}, u32[]{:S(2)}) collective-permute-start(bf16[264,128]{1,0:T(8,128)(2,1)S(1)} %get-tuple-element.93.message.m1), channel_id=1, source_target_pairs={{0,32},{32,0},{64,96},{96,64},{1,33},{33,1},{65,97},{97,65},{2,34}... | collective-permute-start | bytes 202760 | tf_op jit(solution)/shard_map/ppermute | solution.py:347
  158.9 13.8 %all-to-all-start.5 = ((bf16[16,136,128]{2,1,0:T(8,128)(2,1)}), bf16[16,136,128]{2,1,0:T(8,128)(2,1)S(1)}, u32[]{:S(2)}, u32[]{:S(2)}) async-start(bf16[16,136,128]{2,1,0:T(8,128)(2,1)} %shard_map.101), calls=%async_computation.5 | async-start | bytes 1114112 | tf_op jit(solution)/shard_map/all_to_all | solution.py:351
  195.0 5.1 %collective-permute-start.23 = (bf16[264,128]{1,0:T(8,128)(2,1)S(1)}, bf16[264,128]{1,0:T(8,128)(2,1)S(1)}, u32[]{:S(2)}, u32[]{:S(2)}) collective-permute-start(bf16[264,128]{1,0:T(8,128)(2,1)S(1)} %shard_map.107), channel_id=1, source_target_pairs={{0,32},{32,0},{64,96},{96,64},{1,33},{33,1},{65,97},{97,65},{2,34}... | collective-permute-start | bytes 202760 | tf_op jit(solution)/shard_map/ppermute | solution.py:347
  195.6 5.5 %collective-permute-start.22 = (bf16[264,128]{1,0:T(8,128)(2,1)S(1)}, bf16[264,128]{1,0:T(8,128)(2,1)S(1)}, u32[]{:S(2)}, u32[]{:S(2)}) collective-permute-start(bf16[264,128]{1,0:T(8,128)(2,1)S(1)} %shard_map.106), channel_id=1, source_target_pairs={{0,96},{32,64},{64,32},{96,0},{1,97},{33,65},{65,33},{97,1},{2,98}... | collective-permute-start | bytes 202760 | tf_op jit(solution)/shard_map/ppermute | solution.py:347
  197.1 10.2 %slice-start.2 = ((s8[8388608]{0:T(1024)(128)(4,1)}), s8[4194304]{0:T(1024)(128)(4,1)S(1)}, s32[]{:S(2)}) async-start(s8[8388608]{0:T(1024)(128)(4,1)} %bitcast.14), calls=%async_computation.11 | async-start | bytes 8388608
  197.1 12.0 %slice-start.6 = ((s8[8388608]{0:T(1024)(128)(4,1)}), s8[4194304]{0:T(1024)(128)(4,1)S(1)}, s32[]{:S(2)}) async-start(s8[8388608]{0:T(1024)(128)(4,1)} %bitcast.18), calls=%async_computation.15 | async-start | bytes 8388608
  197.1 10.2 %slice-start.3 = ((s8[8388608]{0:T(1024)(128)(4,1)}), s8[4194304]{0:T(1024)(128)(4,1)S(1)}, s32[]{:S(2)}) async-start(s8[8388608]{0:T(1024)(128)(4,1)} %bitcast.14), calls=%async_computation.12 | async-start | bytes 8388608
  197.1 12.0 %slice-start.7 = ((s8[8388608]{0:T(1024)(128)(4,1)}), s8[4194304]{0:T(1024)(128)(4,1)S(1)}, s32[]{:S(2)}) async-start(s8[8388608]{0:T(1024)(128)(4,1)} %bitcast.18), calls=%async_computation.16 | async-start | bytes 8388608
  197.1 5.9 %collective-permute-start.21 = (bf16[264,128]{1,0:T(8,128)(2,1)S(1)}, bf16[264,128]{1,0:T(8,128)(2,1)S(1)}, u32[]{:S(2)}, u32[]{:S(2)}) collective-permute-start(bf16[264,128]{1,0:T(8,128)(2,1)S(1)} %get-tuple-element.103), channel_id=1, source_target_pairs={{0,64},{32,96},{64,0},{96,32},{1,65},{33,97},{65,1},{97,33},{2,66}... | collective-permute-start | bytes 202760 | tf_op jit(solution)/shard_map/ppermute | solution.py:347
  203.2 5.9 %collective-permute-start.26 = (bf16[264,128]{1,0:T(8,128)(2,1)S(1)}, bf16[264,128]{1,0:T(8,128)(2,1)S(1)}, u32[]{:S(2)}, u32[]{:S(2)}) collective-permute-start(bf16[264,128]{1,0:T(8,128)(2,1)S(1)} %get-tuple-element.106.message.m1), channel_id=1, source_target_pairs={{0,64},{32,96},{64,0},{96,32},{1,65},{33,97},{65,1},{97,33},{2,66}... | collective-permute-start | bytes 202760 | tf_op jit(solution)/shard_map/ppermute | solution.py:347
  205.4 5.5 %collective-permute-start.25 = (bf16[264,128]{1,0:T(8,128)(2,1)S(1)}, bf16[264,128]{1,0:T(8,128)(2,1)S(1)}, u32[]{:S(2)}, u32[]{:S(2)}) collective-permute-start(bf16[264,128]{1,0:T(8,128)(2,1)S(1)} %get-tuple-element.106.message.m1), channel_id=1, source_target_pairs={{0,96},{32,64},{64,32},{96,0},{1,97},{33,65},{65,33},{97,1},{2,98}... | collective-permute-start | bytes 202760 | tf_op jit(solution)/shard_map/ppermute | solution.py:347
  207.3 4.5 %collective-permute-start.24 = (bf16[264,128]{1,0:T(8,128)(2,1)S(1)}, bf16[264,128]{1,0:T(8,128)(2,1)S(1)}, u32[]{:S(2)}, u32[]{:S(2)}) collective-permute-start(bf16[264,128]{1,0:T(8,128)(2,1)S(1)} %get-tuple-element.106.message.m1), channel_id=1, source_target_pairs={{0,32},{32,0},{64,96},{96,64},{1,33},{33,1},{65,97},{97,65},{2,34}... | collective-permute-start | bytes 202760 | tf_op jit(solution)/shard_map/ppermute | solution.py:347
  226.3 5.2 %collective-permute-start.27 = (f32[8,128]{1,0:T(8,128)S(1)}, f32[8,128]{1,0:T(8,128)S(1)}, u32[]{:S(2)}, u32[]{:S(2)}) collective-permute-start(f32[8,128]{1,0:T(8,128)S(1)} %get-tuple-element.108.mine), channel_id=1, source_target_pairs={{0,64},{32,96},{64,0},{96,32},{1,65},{33,97},{65,1},{97,33},{2,66}... | collective-permute-start | bytes 12296 | tf_op jit(solution)/shard_map/ppermute | solution.py:347
  227.7 3.8 %collective-permute-start.28 = (f32[8,128]{1,0:T(8,128)S(1)}, f32[8,128]{1,0:T(8,128)S(1)}, u32[]{:S(2)}, u32[]{:S(2)}) collective-permute-start(f32[8,128]{1,0:T(8,128)S(1)} %get-tuple-element.108.mine), channel_id=1, source_target_pairs={{0,32},{32,0},{64,96},{96,64},{1,33},{33,1},{65,97},{97,65},{2,34}... | collective-permute-start | bytes 12296 | tf_op jit(solution)/shard_map/ppermute | solution.py:347
  229.2 4.8 %collective-permute-start.29 = (f32[8,128]{1,0:T(8,128)S(1)}, f32[8,128]{1,0:T(8,128)S(1)}, u32[]{:S(2)}, u32[]{:S(2)}) collective-permute-start(f32[8,128]{1,0:T(8,128)S(1)} %get-tuple-element.108.mine), channel_id=1, source_target_pairs={{0,96},{32,64},{64,32},{96,0},{1,97},{33,65},{65,33},{97,1},{2,98}... | collective-permute-start | bytes 12296 | tf_op jit(solution)/shard_map/ppermute | solution.py:347
  234.7 11.1 %all-to-all-start.8 = ((f32[16,8,128]{2,1,0:T(8,128)}), f32[16,8,128]{2,1,0:T(8,128)S(1)}, u32[]{:S(2)}, u32[]{:S(2)}) async-start(f32[16,8,128]{2,1,0:T(8,128)} %shard_map.114), calls=%async_computation.8 | async-start | bytes 131072 | tf_op jit(solution)/shard_map/all_to_all | solution.py:351
  245.9 1.4 collective-permute-start.30
  (3 other events, 11.5 us)

commit v3 on v2

--- a/solution.py
+++ b/solution.py
@@ -305,26 +305,23 @@
     put_all(message, res[...] - per_frame(about[0:1], RO) * value, squares(value))
 
 
-def image_last_body(arrived, previous, last, image, gamma, beta, norm):
+def image_last_body(arrived, previous, last, image, gamma, beta, norms):
     value, row = gathered(arrived)
     ratio = row / last[0:1]
     value = value + per_frame(ratio, RO) * previous[...]
     image[...] = value
     gamma[...] = wide(row)
     beta[...] = wide(ratio)
-    norm[...] = wide(squares(value))
-
-
-def norm_body(mine, far, near, back, norms):
-    total = mine[...] + far[...] + near[...] + back[...]
-    for c in range(NC):
-        norms[c] = total
+    rows = as_rows(squares(value))
+    for i in range(NX * NC):
+        norms[i] = rows
 
 
 def final_body(k, norms, gamma, search, beta, way, vol, res, image, mine, other, volume):
-    total = norms[0, 0:1]
-    for c in range(1, NC):
-        total = total + norms[c, 0:1]
+    total = norms[0].astype(F32)
+    for i in range(1, NX * NC):
+        total = total + norms[i].astype(F32)
+    total = jnp.sum(total, axis=0, keepdims=True)
     alpha = per_frame(gamma[0:1] / total, VS)
     along = search[...] + per_frame(beta[0:1], VS) * way[...]
     volume[...] = vol[...] + alpha * along
@@ -453,16 +450,16 @@
                 (rays, line, line, column),
                 (arrived, residual, guess, image, gamma),
             )
-    image, gamma, beta, norm = kernel(
-        image_last_body, (rays, line, line, line), (arrived, image, gamma)
-    )
-    others = tuple(swapped(norm, "x", j) for j in (2, 1, 3))
-    norms = kernel(norm_body, shape((NC, *LINE), F32), (norm, *others))
+    image, gamma, beta, norms = kernel(
+        image_last_body,
+        (rays, line, line, shape((NX * NC, PAD, LANES), BF)),
+        (arrived, image, gamma),
+    )
     both = shape((FH, VH + RS), F32)
     mine, other = kernel(
         final_body,
         (both, both),
-        (k, exchanged(norms, COL), gamma, search, beta, direction, volume, residual, image),
+        (k, exchanged(norms, ("x", *COL)), gamma, search, beta, direction, volume, residual, image),
         (pltpu.VMEM((FH, VS), F32),),
     )
     volume, residual = kernel(

time: 250 us -> 247 us (0.988)
    ppermute x31 -> x28, starting transfers between devices: 37.4 us -> 33.2 us  [swapped(): lax.ppermute(value, axis, [(i, i ^ by) for i in range(lax.axis_size(axis))])]
    ppermute x31 -> x28, waiting for transfers between devices: 23.7 us -> 20.2 us  [swapped(): lax.ppermute(value, axis, [(i, i ^ by) for i in range(lax.axis_size(axis))])]
    pallas_call x48 -> x47, Pallas kernels: 32.6 us -> 32.6 us  [kernel(): pl.pallas_call(body, out_shape=outs, in_specs=[smem() if a.dtype == jnp.i...]
  transfers between devices with their start and end apart: 34 -> 31, of which waited for: 21 -> 19; matrix products, arithmetic and copies ran while one was open for 0% -> 0% of each run, Pallas kernels for 8% -> 8%
where the time goes in v3:
time: 247 us; the launch traced here: 245 us
  blocking collectives  90.2 us (37%)
  waiting for transfers between devices  50.5 us (20%)
  starting transfers between devices  45.9 us (19%)
  Pallas kernels  43 us (17%)
  local copies, waits for them, and re-layouts  12.5 us (5%)
    all_to_all x6, blocking collectives, exchanged(): return lax.all_to_all(parts, axis, split_axis=0, concat_axis=0, tiled=True)  90.2 us
    ppermute x28, starting transfers between devices, swapped(): lax.ppermute(value, axis, [(i, i ^ by) for i in range(lax.axis_size(axis))])  33.2 us
    pallas_call x47, Pallas kernels, kernel(): pl.pallas_call(body, out_shape=outs, in_specs=[smem() if a.dtype == jnp.i...  32.6 us
    all_to_all x3, waiting for transfers between devices, exchanged(): return lax.all_to_all(parts, axis, split_axis=0, concat_axis=0, tiled=True)  30.3 us
    ppermute x28, waiting for transfers between devices, swapped(): lax.ppermute(value, axis, [(i, i ^ by) for i in range(lax.axis_size(axis))])  20.2 us
    all_to_all x3, starting transfers between devices, exchanged(): return lax.all_to_all(parts, axis, split_axis=0, concat_axis=0, tiled=True)  12.7 us
    unnamed x34, local copies, waits for them, and re-layouts  12.4 us
    pallas_call x2, Pallas kernels, turned_half(): pl.pallas_call(functools.partial(turned_body, half), out_shape=pltpu.VMEM...  5.53 us
  transfers between devices with their start and end apart: 31, of which 19 were waited for; matrix products, arithmetic and copies ran while one was open for 0% of the time, Pallas kernels for 8%

profile of v3, /device:TPU:0, one launch (start us, length us, event | category | flops | bytes accessed | tf_op | source)
XLA Modules:
  0.0 244.7 jit_solution(9859123110177130676)
XLA Ops:
  5.0 20.4 %all_to_all.45.after.arrived = bf16[16,136,128]{2,1,0:T(8,128)(2,1)} all-to-all(bf16[16,136,128]{2,1,0:T(8,128)(2,1)S(1)} %get-tuple-element.66), channel_id=1, replica_groups=mesh['x'=4,'k'=2,'y'=4,'z'=4] {'y','z'}, dimensions={0} | all-to-all | bytes 1114112 | tf_op jit(solution)/shard_map/all_to_all | solution.py:348
  25.4 4.8 %build.1.dense = bf16[4096,2048]{1,0:T(8,128)(2,1)S(1)} custom-call(s32[1]{0:T(128)} %bitcast.6.x, s32[3,128]{1,0:T(4,128)} %copy-done.7, s32[3,128]{1,0:T(4,128)} %copy-done.8, bf16[128,128,128]{2,1,0:T(8,128)(2,1)} %bitcast.22, bf16[128,128,128]{2,1,0:T(8,128)(2,1)} %collective-permute-done.2.tiles2, bf16[16,136,128]{2,1,0:T(8,128)(2,1)} %all_to_all.45.after.arrived), custom_call_target="tpu_custom_call" | custom-call | tf_op jit(solution)/shard_map/build/pallas_call | solution.py:153
  33.7 1.7 collective-permute-start.4
  35.4 1.6 collective-permute-start.3
  37.8 1.8 collective-permute-done.4.p2
  39.7 1.5 collective-permute-done.3.p1
  41.3 1.7 collective-permute-start.8
  43.0 1.6 collective-permute-start.7
  44.9 2.7 %shard_map.75.turned = bf16[1024,4096]{1,0:T(8,128)(2,1)S(1)} custom-call(bf16[4096,2048]{1,0:T(8,128)(2,1)S(1)} %build.1.dense), custom_call_target="tpu_custom_call" | custom-call | tf_op jit(solution)/shard_map/pallas_call | solution.py:176
  47.6 2.8 %shard_map.76.turned = bf16[1024,4096]{1,0:T(8,128)(2,1)S(1)} custom-call(bf16[4096,2048]{1,0:T(8,128)(2,1)S(1)} %build.1.dense), custom_call_target="tpu_custom_call" | custom-call | tf_op jit(solution)/shard_map/pallas_call | solution.py:176
  53.9 15.0 %all_to_all.46.arrived = bf16[16,136,128]{2,1,0:T(8,128)(2,1)S(1)} all-to-all(bf16[16,136,128]{2,1,0:T(8,128)(2,1)S(1)} %shard_map.80), channel_id=1, replica_groups=mesh['x'=4,'k'=2,'y'=4,'z'=4] {'y','z'}, dimensions={0} | all-to-all | bytes 1114112 | tf_op jit(solution)/shard_map/all_to_all | solution.py:348
  69.2 13.5 %all_to_all.47.arrived = bf16[16,136,128]{2,1,0:T(8,128)(2,1)S(1)} all-to-all(bf16[16,136,128]{2,1,0:T(8,128)(2,1)S(1)} %get-tuple-element.76), channel_id=1, replica_groups=mesh['x'=4,'k'=2,'y'=4,'z'=4] {'y','z'}, dimensions={0} | all-to-all | bytes 1114112 | tf_op jit(solution)/shard_map/all_to_all | solution.py:348
  85.3 1.9 collective-permute-start.11
  87.8 1.8 collective-permute-start.9
  90.5 2.3 collective-permute-done.10.p2
  92.8 1.0 collective-permute-done.9.p1
  94.0 1.7 collective-permute-start.14
  95.7 1.5 collective-permute-start.13
  98.4 1.5 collective-permute-done.14.message.m2
  102.1 1.7 shard_map.90
  103.8 3.6 %all-to-all-start.3 = ((bf16[16,136,128]{2,1,0:T(8,128)(2,1)}), bf16[16,136,128]{2,1,0:T(8,128)(2,1)S(1)}, u32[]{:S(2)}, u32[]{:S(2)}) async-start(bf16[16,136,128]{2,1,0:T(8,128)(2,1)} %shard_map.90), calls=%async_computation.3 | async-start | bytes 1114112 | tf_op jit(solution)/shard_map/all_to_all | solution.py:348
  107.5 10.5 %all-to-all-done.3.arrived = bf16[16,136,128]{2,1,0:T(8,128)(2,1)S(1)} async-done(((bf16[16,136,128]{2,1,0:T(8,128)(2,1)}), bf16[16,136,128]{2,1,0:T(8,128)(2,1)S(1)}, u32[]{:S(2)}, u32[]{:S(2)}) %all-to-all-start.3) | async-done | bytes 557088 | tf_op jit(solution)/shard_map/all_to_all | solution.py:348
  118.2 14.0 %all_to_all.48.arrived = bf16[16,136,128]{2,1,0:T(8,128)(2,1)S(1)} all-to-all(bf16[16,136,128]{2,1,0:T(8,128)(2,1)S(1)} %get-tuple-element.87), channel_id=1, replica_groups=mesh['x'=4,'k'=2,'y'=4,'z'=4] {'y','z'}, dimensions={0} | all-to-all | bytes 1114112 | tf_op jit(solution)/shard_map/all_to_all | solution.py:348
  132.2 5.8 %copy-done.1 = bf16[4096,2048]{1,0:T(8,128)(2,1)S(1)} copy-done((bf16[4096,2048]{1,0:T(8,128)(2,1)S(1)}, bf16[4096,2048]{1,0:T(8,128)(2,1)}, u32[]{:S(2)}) %copy-start.1) | copy-done | bytes 16777240
  141.0 1.6 collective-permute-start.16
  142.7 2.1 collective-permute-start.15
  145.6 0.9 collective-permute-done.16.p2
  146.5 2.0 collective-permute-done.15.p1
  148.8 2.1 collective-permute-start.20
  150.9 1.9 collective-permute-start.19
  153.6 1.0 collective-permute-done.20.message.m2
  157.2 1.7 shard_map.101
  158.9 3.6 %all-to-all-start.5 = ((bf16[16,136,128]{2,1,0:T(8,128)(2,1)}), bf16[16,136,128]{2,1,0:T(8,128)(2,1)S(1)}, u32[]{:S(2)}, u32[]{:S(2)}) async-start(bf16[16,136,128]{2,1,0:T(8,128)(2,1)} %shard_map.101), calls=%async_computation.5 | async-start | bytes 1114112 | tf_op jit(solution)/shard_map/all_to_all | solution.py:348
  162.6 10.1 %all-to-all-done.5.arrived = bf16[16,136,128]{2,1,0:T(8,128)(2,1)S(1)} async-done(((bf16[16,136,128]{2,1,0:T(8,128)(2,1)}), bf16[16,136,128]{2,1,0:T(8,128)(2,1)S(1)}, u32[]{:S(2)}, u32[]{:S(2)}) %all-to-all-start.5) | async-done | bytes 557088 | tf_op jit(solution)/shard_map/all_to_all | solution.py:348
  173.0 13.7 %all_to_all.49.arrived = bf16[16,136,128]{2,1,0:T(8,128)(2,1)S(1)} all-to-all(bf16[16,136,128]{2,1,0:T(8,128)(2,1)S(1)} %get-tuple-element.100), channel_id=1, replica_groups=mesh['x'=4,'k'=2,'y'=4,'z'=4] {'y','z'}, dimensions={0} | all-to-all | bytes 1114112 | tf_op jit(solution)/shard_map/all_to_all | solution.py:348
  186.7 5.8 %copy-done.2 = bf16[4096,2048]{1,0:T(8,128)(2,1)S(1)} copy-done((bf16[4096,2048]{1,0:T(8,128)(2,1)S(1)}, bf16[4096,2048]{1,0:T(8,128)(2,1)}, u32[]{:S(2)}) %copy-start.2) | copy-done | bytes 16777240
  195.6 1.5 collective-permute-start.22
  197.1 2.2 collective-permute-start.21
  200.1 0.9 collective-permute-done.22.p2
  201.1 1.9 collective-permute-done.21.p1
  203.1 2.2 collective-permute-start.26
  205.4 1.9 collective-permute-start.25
  208.1 0.9 collective-permute-done.26.message.m2
  209.9 1.0 collective-permute-done.25.message.m3
  212.6 13.5 %all_to_all.50.arrived = bf16[16,136,128]{2,1,0:T(8,128)(2,1)S(1)} all-to-all(bf16[16,136,128]{2,1,0:T(8,128)(2,1)S(1)} %shard_map.112), channel_id=1, replica_groups=mesh['x'=4,'k'=2,'y'=4,'z'=4] {'y','z'}, dimensions={0} | all-to-all | bytes 1114112 | tf_op jit(solution)/shard_map/all_to_all | solution.py:348
  227.0 5.5 %all-to-all-start.8 = ((bf16[64,8,128]{2,1,0:T(8,128)(2,1)}), bf16[64,8,128]{2,1,0:T(8,128)(2,1)S(1)}, u32[]{:S(2)}, u32[]{:S(2)}) async-start(bf16[64,8,128]{2,1,0:T(8,128)(2,1)} %get-tuple-element.108), calls=%async_computation.8 | async-start | bytes 262144 | tf_op jit(solution)/shard_map/all_to_all | solution.py:348
  232.6 9.7 %all-to-all-done.8.norms = bf16[64,8,128]{2,1,0:T(8,128)(2,1)S(1)} async-done(((bf16[64,8,128]{2,1,0:T(8,128)(2,1)}), bf16[64,8,128]{2,1,0:T(8,128)(2,1)S(1)}, u32[]{:S(2)}, u32[]{:S(2)}) %all-to-all-start.8) | async-done | bytes 131104 | tf_op jit(solution)/shard_map/all_to_all | solution.py:348
  242.6 1.3 collective-permute-done.27.other
  (110 shorter events, 37.4 us)
Async XLA Ops:
  0.6 0.8 copy-start.6
  1.6 2.9 %collective-permute-start = (f32[64,128]{1,0:T(8,128)S(1)}, f32[64,128]{1,0:T(8,128)S(1)}, u32[]{:S(2)}, u32[]{:S(2)}) collective-permute-start(f32[64,128]{1,0:T(8,128)S(1)} %get-tuple-element.64), channel_id=1, source_target_pairs={{0,16},{16,0},{1,17},{17,1},{2,18},{18,2},{3,19},{19,3},{4,20},{20... | collective-permute-start | bytes 98312 | tf_op jit(solution)/shard_map/ppermute | solution.py:344
  3.1 22.2 %copy-start.7 = (s32[3,128]{1,0:T(4,128)}, s32[3,128]{1,0:T(4,128)S(1)}, u32[]{:S(2)}) copy-start(s32[3,128]{1,0:T(4,128)S(1)} %add_add_fusion.table) | copy-start | bytes 4612
  3.1 1.3 collective-permute-start.1
  4.5 20.9 %copy-start.8 = (s32[3,128]{1,0:T(4,128)}, s32[3,128]{1,0:T(4,128)S(1)}, u32[]{:S(2)}) copy-start(s32[3,128]{1,0:T(4,128)S(1)} %collective-permute-done.1.table2) | copy-start | bytes 4612
  4.5 20.9 %collective-permute-start.2 = (bf16[128,128,128]{2,1,0:T(8,128)(2,1)}, bf16[128,128,128]{2,1,0:T(8,128)(2,1)}, u32[]{:S(2)}, u32[]{:S(2)}) collective-permute-start(bf16[128,128,128]{2,1,0:T(8,128)(2,1)} %bitcast.21), channel_id=1, source_target_pairs={{0,16},{16,0},{1,17},{17,1},{2,18},{18,2},{3,19},{19,3},{4,20},{20... | collective-permute-start | bytes 12582920 | tf_op jit(solution)/shard_map/ppermute | solution.py:344
  25.4 4.9 %copy-start.5 = (bf16[16,136,128]{2,1,0:T(8,128)(2,1)S(1)}, bf16[16,136,128]{2,1,0:T(8,128)(2,1)}, u32[]{:S(2)}) copy-start(bf16[16,136,128]{2,1,0:T(8,128)(2,1)} %all_to_all.45.after.arrived) | copy-start | bytes 1671172
  30.2 59.4 %copy-start = (bf16[4096,2048]{1,0:T(8,128)(2,1)}, bf16[4096,2048]{1,0:T(8,128)(2,1)S(1)}, u32[]{:S(2)}) copy-start(bf16[4096,2048]{1,0:T(8,128)(2,1)S(1)} %build.1.dense) | copy-start | bytes 50331652
  32.8 5.0 %collective-permute-start.5 = (bf16[264,128]{1,0:T(8,128)(2,1)S(1)}, bf16[264,128]{1,0:T(8,128)(2,1)S(1)}, u32[]{:S(2)}, u32[]{:S(2)}) collective-permute-start(bf16[264,128]{1,0:T(8,128)(2,1)S(1)} %shard_map.73), channel_id=1, source_target_pairs={{0,32},{32,0},{64,96},{96,64},{1,33},{33,1},{65,97},{97,65},{2,34}... | collective-permute-start | bytes 202760 | tf_op jit(solution)/shard_map/ppermute | solution.py:344
  33.7 6.0 %collective-permute-start.4 = (bf16[264,128]{1,0:T(8,128)(2,1)S(1)}, bf16[264,128]{1,0:T(8,128)(2,1)S(1)}, u32[]{:S(2)}, u32[]{:S(2)}) collective-permute-start(bf16[264,128]{1,0:T(8,128)(2,1)S(1)} %shard_map.72), channel_id=1, source_target_pairs={{0,96},{32,64},{64,32},{96,0},{1,97},{33,65},{65,33},{97,1},{2,98}... | collective-permute-start | bytes 202760 | tf_op jit(solution)/shard_map/ppermute | solution.py:344
  35.4 5.8 %collective-permute-start.3 = (bf16[264,128]{1,0:T(8,128)(2,1)S(1)}, bf16[264,128]{1,0:T(8,128)(2,1)S(1)}, u32[]{:S(2)}, u32[]{:S(2)}) collective-permute-start(bf16[264,128]{1,0:T(8,128)(2,1)S(1)} %get-tuple-element.72), channel_id=1, source_target_pairs={{0,64},{32,96},{64,0},{96,32},{1,65},{33,97},{65,1},{97,33},{2,66}... | collective-permute-start | bytes 202760 | tf_op jit(solution)/shard_map/ppermute | solution.py:344
  41.3 10.0 %collective-permute-start.8 = (bf16[264,128]{1,0:T(8,128)(2,1)S(1)}, bf16[264,128]{1,0:T(8,128)(2,1)S(1)}, u32[]{:S(2)}, u32[]{:S(2)}) collective-permute-start(bf16[264,128]{1,0:T(8,128)(2,1)S(1)} %get-tuple-element.73.message.m1), channel_id=1, source_target_pairs={{0,64},{32,96},{64,0},{96,32},{1,65},{33,97},{65,1},{97,33},{2,66}... | collective-permute-start | bytes 202760 | tf_op jit(solution)/shard_map/ppermute | solution.py:344
  43.0 9.2 %collective-permute-start.7 = (bf16[264,128]{1,0:T(8,128)(2,1)S(1)}, bf16[264,128]{1,0:T(8,128)(2,1)S(1)}, u32[]{:S(2)}, u32[]{:S(2)}) collective-permute-start(bf16[264,128]{1,0:T(8,128)(2,1)S(1)} %get-tuple-element.73.message.m1), channel_id=1, source_target_pairs={{0,96},{32,64},{64,32},{96,0},{1,97},{33,65},{65,33},{97,1},{2,98}... | collective-permute-start | bytes 202760 | tf_op jit(solution)/shard_map/ppermute | solution.py:344
  44.6 8.4 %collective-permute-start.6 = (bf16[264,128]{1,0:T(8,128)(2,1)S(1)}, bf16[264,128]{1,0:T(8,128)(2,1)S(1)}, u32[]{:S(2)}, u32[]{:S(2)}) collective-permute-start(bf16[264,128]{1,0:T(8,128)(2,1)S(1)} %get-tuple-element.73.message.m1), channel_id=1, source_target_pairs={{0,32},{32,0},{64,96},{96,64},{1,33},{33,1},{65,97},{97,65},{2,34}... | collective-permute-start | bytes 202760 | tf_op jit(solution)/shard_map/ppermute | solution.py:344
  47.6 54.5 %copy-start.3 = (bf16[1024,4096]{1,0:T(8,128)(2,1)}, bf16[1024,4096]{1,0:T(8,128)(2,1)S(1)}, u32[]{:S(2)}) copy-start(bf16[1024,4096]{1,0:T(8,128)(2,1)S(1)} %shard_map.75.turned) | copy-start | bytes 25165828
  50.5 50.8 %copy-start.4 = (bf16[1024,4096]{1,0:T(8,128)(2,1)}, bf16[1024,4096]{1,0:T(8,128)(2,1)S(1)}, u32[]{:S(2)}) copy-start(bf16[1024,4096]{1,0:T(8,128)(2,1)S(1)} %shard_map.76.turned) | copy-start | bytes 25165828
  85.3 5.2 %collective-permute-start.11 = (bf16[264,128]{1,0:T(8,128)(2,1)S(1)}, bf16[264,128]{1,0:T(8,128)(2,1)S(1)}, u32[]{:S(2)}, u32[]{:S(2)}) collective-permute-start(bf16[264,128]{1,0:T(8,128)(2,1)S(1)} %shard_map.85), channel_id=1, source_target_pairs={{0,32},{32,0},{64,96},{96,64},{1,33},{33,1},{65,97},{97,65},{2,34}... | collective-permute-start | bytes 202760 | tf_op jit(solution)/shard_map/ppermute | solution.py:344
  87.2 5.6 %collective-permute-start.10 = (bf16[264,128]{1,0:T(8,128)(2,1)S(1)}, bf16[264,128]{1,0:T(8,128)(2,1)S(1)}, u32[]{:S(2)}, u32[]{:S(2)}) collective-permute-start(bf16[264,128]{1,0:T(8,128)(2,1)S(1)} %shard_map.84), channel_id=1, source_target_pairs={{0,96},{32,64},{64,32},{96,0},{1,97},{33,65},{65,33},{97,1},{2,98}... | collective-permute-start | bytes 202760 | tf_op jit(solution)/shard_map/ppermute | solution.py:344
  87.8 6.0 %collective-permute-start.9 = (bf16[264,128]{1,0:T(8,128)(2,1)S(1)}, bf16[264,128]{1,0:T(8,128)(2,1)S(1)}, u32[]{:S(2)}, u32[]{:S(2)}) collective-permute-start(bf16[264,128]{1,0:T(8,128)(2,1)S(1)} %get-tuple-element.79), channel_id=1, source_target_pairs={{0,64},{32,96},{64,0},{96,32},{1,65},{33,97},{65,1},{97,33},{2,66}... | collective-permute-start | bytes 202760 | tf_op jit(solution)/shard_map/ppermute | solution.py:344
  94.0 5.9 %collective-permute-start.14 = (bf16[264,128]{1,0:T(8,128)(2,1)S(1)}, bf16[264,128]{1,0:T(8,128)(2,1)S(1)}, u32[]{:S(2)}, u32[]{:S(2)}) collective-permute-start(bf16[264,128]{1,0:T(8,128)(2,1)S(1)} %get-tuple-element.83.message.m1), channel_id=1, source_target_pairs={{0,64},{32,96},{64,0},{96,32},{1,65},{33,97},{65,1},{97,33},{2,66}... | collective-permute-start | bytes 202760 | tf_op jit(solution)/shard_map/ppermute | solution.py:344
  95.7 5.5 %collective-permute-start.13 = (bf16[264,128]{1,0:T(8,128)(2,1)S(1)}, bf16[264,128]{1,0:T(8,128)(2,1)S(1)}, u32[]{:S(2)}, u32[]{:S(2)}) collective-permute-start(bf16[264,128]{1,0:T(8,128)(2,1)S(1)} %get-tuple-element.83.message.m1), channel_id=1, source_target_pairs={{0,96},{32,64},{64,32},{96,0},{1,97},{33,65},{65,33},{97,1},{2,98}... | collective-permute-start | bytes 202760 | tf_op jit(solution)/shard_map/ppermute | solution.py:344
  97.2 4.9 %collective-permute-start.12 = (bf16[264,128]{1,0:T(8,128)(2,1)S(1)}, bf16[264,128]{1,0:T(8,128)(2,1)S(1)}, u32[]{:S(2)}, u32[]{:S(2)}) collective-permute-start(bf16[264,128]{1,0:T(8,128)(2,1)S(1)} %get-tuple-element.83.message.m1), channel_id=1, source_target_pairs={{0,32},{32,0},{64,96},{96,64},{1,33},{33,1},{65,97},{97,65},{2,34}... | collective-permute-start | bytes 202760 | tf_op jit(solution)/shard_map/ppermute | solution.py:344
  103.8 14.2 %all-to-all-start.3 = ((bf16[16,136,128]{2,1,0:T(8,128)(2,1)}), bf16[16,136,128]{2,1,0:T(8,128)(2,1)S(1)}, u32[]{:S(2)}, u32[]{:S(2)}) async-start(bf16[16,136,128]{2,1,0:T(8,128)(2,1)} %shard_map.90), calls=%async_computation.3 | async-start | bytes 1114112 | tf_op jit(solution)/shard_map/all_to_all | solution.py:348
  132.2 5.8 %copy-start.1 = (bf16[4096,2048]{1,0:T(8,128)(2,1)S(1)}, bf16[4096,2048]{1,0:T(8,128)(2,1)}, u32[]{:S(2)}) copy-start(bf16[4096,2048]{1,0:T(8,128)(2,1)} %copy-done) | copy-start | bytes 50331652
  140.5 5.1 %collective-permute-start.17 = (bf16[264,128]{1,0:T(8,128)(2,1)S(1)}, bf16[264,128]{1,0:T(8,128)(2,1)S(1)}, u32[]{:S(2)}, u32[]{:S(2)}) collective-permute-start(bf16[264,128]{1,0:T(8,128)(2,1)S(1)} %shard_map.96), channel_id=1, source_target_pairs={{0,32},{32,0},{64,96},{96,64},{1,33},{33,1},{65,97},{97,65},{2,34}... | collective-permute-start | bytes 202760 | tf_op jit(solution)/shard_map/ppermute | solution.py:344
  141.0 5.5 %collective-permute-start.16 = (bf16[264,128]{1,0:T(8,128)(2,1)S(1)}, bf16[264,128]{1,0:T(8,128)(2,1)S(1)}, u32[]{:S(2)}, u32[]{:S(2)}) collective-permute-start(bf16[264,128]{1,0:T(8,128)(2,1)S(1)} %shard_map.95), channel_id=1, source_target_pairs={{0,96},{32,64},{64,32},{96,0},{1,97},{33,65},{65,33},{97,1},{2,98}... | collective-permute-start | bytes 202760 | tf_op jit(solution)/shard_map/ppermute | solution.py:344
  142.7 10.1 %slice-start = ((s8[8388608]{0:T(1024)(128)(4,1)}), s8[4194304]{0:T(1024)(128)(4,1)S(1)}, s32[]{:S(2)}) async-start(s8[8388608]{0:T(1024)(128)(4,1)} %bitcast.12), calls=%async_computation.9 | async-start | bytes 8388608
  142.7 12.0 %slice-start.4 = ((s8[8388608]{0:T(1024)(128)(4,1)}), s8[4194304]{0:T(1024)(128)(4,1)S(1)}, s32[]{:S(2)}) async-start(s8[8388608]{0:T(1024)(128)(4,1)} %bitcast.16), calls=%async_computation.13 | async-start | bytes 8388608
  142.7 10.1 %slice-start.1 = ((s8[8388608]{0:T(1024)(128)(4,1)}), s8[4194304]{0:T(1024)(128)(4,1)S(1)}, s32[]{:S(2)}) async-start(s8[8388608]{0:T(1024)(128)(4,1)} %bitcast.12), calls=%async_computation.10 | async-start | bytes 8388608
  142.7 12.0 %slice-start.5 = ((s8[8388608]{0:T(1024)(128)(4,1)}), s8[4194304]{0:T(1024)(128)(4,1)S(1)}, s32[]{:S(2)}) async-start(s8[8388608]{0:T(1024)(128)(4,1)} %bitcast.16), calls=%async_computation.14 | async-start | bytes 8388608
  142.7 5.9 %collective-permute-start.15 = (bf16[264,128]{1,0:T(8,128)(2,1)S(1)}, bf16[264,128]{1,0:T(8,128)(2,1)S(1)}, u32[]{:S(2)}, u32[]{:S(2)}) collective-permute-start(bf16[264,128]{1,0:T(8,128)(2,1)S(1)} %get-tuple-element.90), channel_id=1, source_target_pairs={{0,64},{32,96},{64,0},{96,32},{1,65},{33,97},{65,1},{97,33},{2,66}... | collective-permute-start | bytes 202760 | tf_op jit(solution)/shard_map/ppermute | solution.py:344
  148.8 5.9 %collective-permute-start.20 = (bf16[264,128]{1,0:T(8,128)(2,1)S(1)}, bf16[264,128]{1,0:T(8,128)(2,1)S(1)}, u32[]{:S(2)}, u32[]{:S(2)}) collective-permute-start(bf16[264,128]{1,0:T(8,128)(2,1)S(1)} %get-tuple-element.93.message.m1), channel_id=1, source_target_pairs={{0,64},{32,96},{64,0},{96,32},{1,65},{33,97},{65,1},{97,33},{2,66}... | collective-permute-start | bytes 202760 | tf_op jit(solution)/shard_map/ppermute | solution.py:344
  150.9 5.5 %collective-permute-start.19 = (bf16[264,128]{1,0:T(8,128)(2,1)S(1)}, bf16[264,128]{1,0:T(8,128)(2,1)S(1)}, u32[]{:S(2)}, u32[]{:S(2)}) collective-permute-start(bf16[264,128]{1,0:T(8,128)(2,1)S(1)} %get-tuple-element.93.message.m1), channel_id=1, source_target_pairs={{0,96},{32,64},{64,32},{96,0},{1,97},{33,65},{65,33},{97,1},{2,98}... | collective-permute-start | bytes 202760 | tf_op jit(solution)/shard_map/ppermute | solution.py:344
  152.8 4.5 %collective-permute-start.18 = (bf16[264,128]{1,0:T(8,128)(2,1)S(1)}, bf16[264,128]{1,0:T(8,128)(2,1)S(1)}, u32[]{:S(2)}, u32[]{:S(2)}) collective-permute-start(bf16[264,128]{1,0:T(8,128)(2,1)S(1)} %get-tuple-element.93.message.m1), channel_id=1, source_target_pairs={{0,32},{32,0},{64,96},{96,64},{1,33},{33,1},{65,97},{97,65},{2,34}... | collective-permute-start | bytes 202760 | tf_op jit(solution)/shard_map/ppermute | solution.py:344
  158.9 13.8 %all-to-all-start.5 = ((bf16[16,136,128]{2,1,0:T(8,128)(2,1)}), bf16[16,136,128]{2,1,0:T(8,128)(2,1)S(1)}, u32[]{:S(2)}, u32[]{:S(2)}) async-start(bf16[16,136,128]{2,1,0:T(8,128)(2,1)} %shard_map.101), calls=%async_computation.5 | async-start | bytes 1114112 | tf_op jit(solution)/shard_map/all_to_all | solution.py:348
  186.7 5.8 %copy-start.2 = (bf16[4096,2048]{1,0:T(8,128)(2,1)S(1)}, bf16[4096,2048]{1,0:T(8,128)(2,1)}, u32[]{:S(2)}) copy-start(bf16[4096,2048]{1,0:T(8,128)(2,1)} %copy-done) | copy-start | bytes 50331652
  195.0 5.1 %collective-permute-start.23 = (bf16[264,128]{1,0:T(8,128)(2,1)S(1)}, bf16[264,128]{1,0:T(8,128)(2,1)S(1)}, u32[]{:S(2)}, u32[]{:S(2)}) collective-permute-start(bf16[264,128]{1,0:T(8,128)(2,1)S(1)} %shard_map.107), channel_id=1, source_target_pairs={{0,32},{32,0},{64,96},{96,64},{1,33},{33,1},{65,97},{97,65},{2,34}... | collective-permute-start | bytes 202760 | tf_op jit(solution)/shard_map/ppermute | solution.py:344
  195.6 5.5 %collective-permute-start.22 = (bf16[264,128]{1,0:T(8,128)(2,1)S(1)}, bf16[264,128]{1,0:T(8,128)(2,1)S(1)}, u32[]{:S(2)}, u32[]{:S(2)}) collective-permute-start(bf16[264,128]{1,0:T(8,128)(2,1)S(1)} %shard_map.106), channel_id=1, source_target_pairs={{0,96},{32,64},{64,32},{96,0},{1,97},{33,65},{65,33},{97,1},{2,98}... | collective-permute-start | bytes 202760 | tf_op jit(solution)/shard_map/ppermute | solution.py:344
  197.0 10.2 %slice-start.2 = ((s8[8388608]{0:T(1024)(128)(4,1)}), s8[4194304]{0:T(1024)(128)(4,1)S(1)}, s32[]{:S(2)}) async-start(s8[8388608]{0:T(1024)(128)(4,1)} %bitcast.14), calls=%async_computation.11 | async-start | bytes 8388608
  197.1 12.0 %slice-start.6 = ((s8[8388608]{0:T(1024)(128)(4,1)}), s8[4194304]{0:T(1024)(128)(4,1)S(1)}, s32[]{:S(2)}) async-start(s8[8388608]{0:T(1024)(128)(4,1)} %bitcast.18), calls=%async_computation.15 | async-start | bytes 8388608
  197.1 10.2 %slice-start.3 = ((s8[8388608]{0:T(1024)(128)(4,1)}), s8[4194304]{0:T(1024)(128)(4,1)S(1)}, s32[]{:S(2)}) async-start(s8[8388608]{0:T(1024)(128)(4,1)} %bitcast.14), calls=%async_computation.12 | async-start | bytes 8388608
  197.1 12.0 %slice-start.7 = ((s8[8388608]{0:T(1024)(128)(4,1)}), s8[4194304]{0:T(1024)(128)(4,1)S(1)}, s32[]{:S(2)}) async-start(s8[8388608]{0:T(1024)(128)(4,1)} %bitcast.18), calls=%async_computation.16 | async-start | bytes 8388608
  197.1 5.9 %collective-permute-start.21 = (bf16[264,128]{1,0:T(8,128)(2,1)S(1)}, bf16[264,128]{1,0:T(8,128)(2,1)S(1)}, u32[]{:S(2)}, u32[]{:S(2)}) collective-permute-start(bf16[264,128]{1,0:T(8,128)(2,1)S(1)} %get-tuple-element.103), channel_id=1, source_target_pairs={{0,64},{32,96},{64,0},{96,32},{1,65},{33,97},{65,1},{97,33},{2,66}... | collective-permute-start | bytes 202760 | tf_op jit(solution)/shard_map/ppermute | solution.py:344
  203.1 5.9 %collective-permute-start.26 = (bf16[264,128]{1,0:T(8,128)(2,1)S(1)}, bf16[264,128]{1,0:T(8,128)(2,1)S(1)}, u32[]{:S(2)}, u32[]{:S(2)}) collective-permute-start(bf16[264,128]{1,0:T(8,128)(2,1)S(1)} %get-tuple-element.106.message.m1), channel_id=1, source_target_pairs={{0,64},{32,96},{64,0},{96,32},{1,65},{33,97},{65,1},{97,33},{2,66}... | collective-permute-start | bytes 202760 | tf_op jit(solution)/shard_map/ppermute | solution.py:344
  205.4 5.5 %collective-permute-start.25 = (bf16[264,128]{1,0:T(8,128)(2,1)S(1)}, bf16[264,128]{1,0:T(8,128)(2,1)S(1)}, u32[]{:S(2)}, u32[]{:S(2)}) collective-permute-start(bf16[264,128]{1,0:T(8,128)(2,1)S(1)} %get-tuple-element.106.message.m1), channel_id=1, source_target_pairs={{0,96},{32,64},{64,32},{96,0},{1,97},{33,65},{65,33},{97,1},{2,98}... | collective-permute-start | bytes 202760 | tf_op jit(solution)/shard_map/ppermute | solution.py:344
  207.2 4.5 %collective-permute-start.24 = (bf16[264,128]{1,0:T(8,128)(2,1)S(1)}, bf16[264,128]{1,0:T(8,128)(2,1)S(1)}, u32[]{:S(2)}, u32[]{:S(2)}) collective-permute-start(bf16[264,128]{1,0:T(8,128)(2,1)S(1)} %get-tuple-element.106.message.m1), channel_id=1, source_target_pairs={{0,32},{32,0},{64,96},{96,64},{1,33},{33,1},{65,97},{97,65},{2,34}... | collective-permute-start | bytes 202760 | tf_op jit(solution)/shard_map/ppermute | solution.py:344
  227.0 15.3 %all-to-all-start.8 = ((bf16[64,8,128]{2,1,0:T(8,128)(2,1)}), bf16[64,8,128]{2,1,0:T(8,128)(2,1)S(1)}, u32[]{:S(2)}, u32[]{:S(2)}) async-start(bf16[64,8,128]{2,1,0:T(8,128)(2,1)} %get-tuple-element.108), calls=%async_computation.8 | async-start | bytes 262144 | tf_op jit(solution)/shard_map/all_to_all | solution.py:348
  242.5 1.4 collective-permute-start.27
